TPU v7x, 16 devices: a 4x2x1 block of a 4x4x8 slice. The times are simulated.
16 devices in a mesh: rep: 2 (over y, z), shard: 8 (over x, core).
Axes of the slice: x: 4, y: 2, z: 1, core: 2. Of those that a mesh axis runs over, the one named last changes fastest.
The devices are a block of a 4x4x8 slice.
Arguments:
- ratings: float32 [1024, 4096], P(('rep', 'shard')), parts along dimension 0
- observed: int32 [1024, 4096], P(('rep', 'shard')), parts along dimension 0
- user_init: float32 [1024, 128], P(('rep', 'shard')), parts along dimension 0
- item_init: float32 [8192, 128], P(('rep', 'shard')), parts along dimension 0
Outputs:
- output 1: float32 [1024, 128], P(('rep', 'shard')), parts along dimension 0
- output 2: float32 [8192, 128], P(('rep', 'shard')), parts along dimension 0
There are 2 independent parts. A program takes and returns all parts, laid end to end along the dimension named above; each array names one.
All inputs are finite; a program needn't handle non-finite values.
Results may differ from a plain program's by a relative error of at most 0.00254815.
Values are sent between devices in bfloat16 or wider.
A program may use at most 768 MiB of HBM per device.

v0:
```python
import jax
import jax.numpy as jnp
import math
from jax import lax
from jax.sharding import PartitionSpec as P

STRATUM_STEPS = 4
EPOCHS = 2


def solution(mesh):
    group_devs = mesh.shape["shard"]
    row_spec = P(("rep", "shard"), None)
    shift_back = [(source, (source - 1) % group_devs) for source in range(group_devs)]

    def local(ratings, observed, user_init, item_init):
        users_dev = ratings.shape[0]
        items_dev, factor_rank = item_init.shape
        step_scale = (users_dev + items_dev + factor_rank) / math.sqrt(factor_rank)
        step_size = 0.5 / step_scale
        weight_decay = 0.03 * math.sqrt(users_dev * items_dev / factor_rank)
        seen_all = observed != 0
        my_index = lax.axis_index("shard")

        def stratum(stratum_idx, state_pair):
            user_blk, item_blk = state_pair
            col_start = ((my_index + stratum_idx) % group_devs) * items_dev
            rating_blk = lax.dynamic_slice_in_dim(ratings, col_start, items_dev, axis=1)
            seen_blk = lax.dynamic_slice_in_dim(seen_all, col_start, items_dev, axis=1)

            def step(unused, inner_pair):
                user_cur, item_cur = inner_pair
                item_bf = item_cur.astype(jnp.bfloat16)
                predicted = jnp.einsum("ur,ir->ui", user_cur.astype(jnp.bfloat16), item_bf, preferred_element_type=jnp.float32)
                residual = jnp.where(seen_blk, predicted - rating_blk, 0.0).astype(jnp.bfloat16)
                grad_user = jnp.dot(residual, item_bf, preferred_element_type=jnp.float32)
                user_new = user_cur - step_size * (grad_user + weight_decay * user_cur)
                user_bf = user_new.astype(jnp.bfloat16)
                predicted = jnp.einsum("ur,ir->ui", user_bf, item_bf, preferred_element_type=jnp.float32)
                residual = jnp.where(seen_blk, predicted - rating_blk, 0.0).astype(jnp.bfloat16)
                grad_item = jnp.einsum("ui,ur->ir", residual, user_bf, preferred_element_type=jnp.float32)
                item_new = item_cur - step_size * (grad_item + weight_decay * item_cur)
                return user_new, item_new

            user_blk, item_blk = lax.fori_loop(0, STRATUM_STEPS, step, (user_blk, item_blk))
            item_blk = lax.ppermute(item_blk, "shard", shift_back)
            return user_blk, item_blk

        return lax.fori_loop(0, EPOCHS * group_devs, stratum, (user_init, item_init))

    return jax.shard_map(local, mesh=mesh, in_specs=(row_spec, row_spec, row_spec, row_spec), out_specs=(row_spec, row_spec), check_vma=False)
```

profile of v0, /device:TPU:112, one launch (start us, length us, event | category | flops | bytes accessed | tf_op | source)
XLA Modules:
  0.0 180.4 jit_solution(5849407703364595334)
XLA Ops:
  2.1 177.6 %while.53 = (s32[]{:T(128)}, f32[64,128]{1,0:T(8,128)S(1)}, f32[512,128]{1,0:T(8,128)S(1)}, s32[]{:T(128)}, f32[64,4096]{1,0:T(8,128)}, /*index=5*/pred[64,4096]...) while((s32[]{:T(128)}, f32[64,128]{1,0:T(8,128)S(1)}, ...), condition=%wide.region_3.4_spmd, body=%wide.region_0.3_spmd.sunk | while | flops 34267152 | bytes 3703249 | solution.py:49
  6.1 3.4 %collective-permute-start = (f32[512,128]{1,0:T(8,128)S(1)}, f32[512,128]{1,0:T(8,128)S(1)}, u32[]{:S(2)}, u32[]{:S(2)}) collective-permute-start(f32[512,128]{1,0:T(8,128)S(1)} %get-tuple-element.291), channel_id=1, source_target_pairs={{0,7},{1,0},{2,1},{3,2},{4,3},{5,4},{6,5},{7,6},{8,15},{9,8},{10,9... | collective-permute-start | bytes 786440 | tf_op jit(solution)/shard_map/while/body/eval_jaxpr/ppermute | solution.py:46
  9.5 3.9 %collective-permute-done = f32[512,128]{1,0:T(8,128)S(1)} collective-permute-done((f32[512,128]{1,0:T(8,128)S(1)}, f32[512,128]{1,0:T(8,128)S(1)}, u32[]{:S(2)}, u32[]{:S(2)}) %collective-permute-start) | collective-permute-done | bytes 262176 | tf_op jit(solution)/shard_map/while/body/eval_jaxpr/ppermute | solution.py:46
  14.4 3.0 %while.54 = (s32[]{:T(128)}, f32[64,128]{1,0:T(8,128)S(1)}, f32[512,128]{1,0:T(8,128)S(1)}, f32[64,512]{1,0:T(8,128)S(1)}, pred[64,512]{1,0:T(32,128)(4,1)S(1)}, /*index=5*/s32[]{:T(128)}) while((s32[]{:T(128)}, f32[64,128]{1,0:T(8,128)S(1)}, f32[512,128]{1,0:T(8,128)S(1)}, f32[64,512]{1,0:T(8,128)S(1)}, pred[64,512]{1,0:T(32,128)(4,1)S(1)}, ...), condition=%wide.region_2.2_spmd, body=%wide.region_1.1_spmd.sunk | while | flops 34267136 | bytes 1802309 | solution.py:45
  17.4 3.2 %collective-permute-start = (f32[512,128]{1,0:T(8,128)S(1)}, f32[512,128]{1,0:T(8,128)S(1)}, u32[]{:S(2)}, u32[]{:S(2)}) collective-permute-start(f32[512,128]{1,0:T(8,128)S(1)} %get-tuple-element.291), channel_id=1, source_target_pairs={{0,7},{1,0},{2,1},{3,2},{4,3},{5,4},{6,5},{7,6},{8,15},{9,8},{10,9... | collective-permute-start | bytes 786440 | tf_op jit(solution)/shard_map/while/body/eval_jaxpr/ppermute | solution.py:46
  20.6 3.9 %collective-permute-done = f32[512,128]{1,0:T(8,128)S(1)} collective-permute-done((f32[512,128]{1,0:T(8,128)S(1)}, f32[512,128]{1,0:T(8,128)S(1)}, u32[]{:S(2)}, u32[]{:S(2)}) %collective-permute-start) | collective-permute-done | bytes 262176 | tf_op jit(solution)/shard_map/while/body/eval_jaxpr/ppermute | solution.py:46
  25.5 3.0 %while.54 = (s32[]{:T(128)}, f32[64,128]{1,0:T(8,128)S(1)}, f32[512,128]{1,0:T(8,128)S(1)}, f32[64,512]{1,0:T(8,128)S(1)}, pred[64,512]{1,0:T(32,128)(4,1)S(1)}, /*index=5*/s32[]{:T(128)}) while((s32[]{:T(128)}, f32[64,128]{1,0:T(8,128)S(1)}, f32[512,128]{1,0:T(8,128)S(1)}, f32[64,512]{1,0:T(8,128)S(1)}, pred[64,512]{1,0:T(32,128)(4,1)S(1)}, ...), condition=%wide.region_2.2_spmd, body=%wide.region_1.1_spmd.sunk | while | flops 34267136 | bytes 1802309 | solution.py:45
  28.5 3.2 %collective-permute-start = (f32[512,128]{1,0:T(8,128)S(1)}, f32[512,128]{1,0:T(8,128)S(1)}, u32[]{:S(2)}, u32[]{:S(2)}) collective-permute-start(f32[512,128]{1,0:T(8,128)S(1)} %get-tuple-element.291), channel_id=1, source_target_pairs={{0,7},{1,0},{2,1},{3,2},{4,3},{5,4},{6,5},{7,6},{8,15},{9,8},{10,9... | collective-permute-start | bytes 786440 | tf_op jit(solution)/shard_map/while/body/eval_jaxpr/ppermute | solution.py:46
  31.7 3.9 %collective-permute-done = f32[512,128]{1,0:T(8,128)S(1)} collective-permute-done((f32[512,128]{1,0:T(8,128)S(1)}, f32[512,128]{1,0:T(8,128)S(1)}, u32[]{:S(2)}, u32[]{:S(2)}) %collective-permute-start) | collective-permute-done | bytes 262176 | tf_op jit(solution)/shard_map/while/body/eval_jaxpr/ppermute | solution.py:46
  36.6 3.0 %while.54 = (s32[]{:T(128)}, f32[64,128]{1,0:T(8,128)S(1)}, f32[512,128]{1,0:T(8,128)S(1)}, f32[64,512]{1,0:T(8,128)S(1)}, pred[64,512]{1,0:T(32,128)(4,1)S(1)}, /*index=5*/s32[]{:T(128)}) while((s32[]{:T(128)}, f32[64,128]{1,0:T(8,128)S(1)}, f32[512,128]{1,0:T(8,128)S(1)}, f32[64,512]{1,0:T(8,128)S(1)}, pred[64,512]{1,0:T(32,128)(4,1)S(1)}, ...), condition=%wide.region_2.2_spmd, body=%wide.region_1.1_spmd.sunk | while | flops 34267136 | bytes 1802309 | solution.py:45
  39.6 3.2 %collective-permute-start = (f32[512,128]{1,0:T(8,128)S(1)}, f32[512,128]{1,0:T(8,128)S(1)}, u32[]{:S(2)}, u32[]{:S(2)}) collective-permute-start(f32[512,128]{1,0:T(8,128)S(1)} %get-tuple-element.291), channel_id=1, source_target_pairs={{0,7},{1,0},{2,1},{3,2},{4,3},{5,4},{6,5},{7,6},{8,15},{9,8},{10,9... | collective-permute-start | bytes 786440 | tf_op jit(solution)/shard_map/while/body/eval_jaxpr/ppermute | solution.py:46
  42.8 3.9 %collective-permute-done = f32[512,128]{1,0:T(8,128)S(1)} collective-permute-done((f32[512,128]{1,0:T(8,128)S(1)}, f32[512,128]{1,0:T(8,128)S(1)}, u32[]{:S(2)}, u32[]{:S(2)}) %collective-permute-start) | collective-permute-done | bytes 262176 | tf_op jit(solution)/shard_map/while/body/eval_jaxpr/ppermute | solution.py:46
  47.6 3.0 %while.54 = (s32[]{:T(128)}, f32[64,128]{1,0:T(8,128)S(1)}, f32[512,128]{1,0:T(8,128)S(1)}, f32[64,512]{1,0:T(8,128)S(1)}, pred[64,512]{1,0:T(32,128)(4,1)S(1)}, /*index=5*/s32[]{:T(128)}) while((s32[]{:T(128)}, f32[64,128]{1,0:T(8,128)S(1)}, f32[512,128]{1,0:T(8,128)S(1)}, f32[64,512]{1,0:T(8,128)S(1)}, pred[64,512]{1,0:T(32,128)(4,1)S(1)}, ...), condition=%wide.region_2.2_spmd, body=%wide.region_1.1_spmd.sunk | while | flops 34267136 | bytes 1802309 | solution.py:45
  50.7 3.2 %collective-permute-start = (f32[512,128]{1,0:T(8,128)S(1)}, f32[512,128]{1,0:T(8,128)S(1)}, u32[]{:S(2)}, u32[]{:S(2)}) collective-permute-start(f32[512,128]{1,0:T(8,128)S(1)} %get-tuple-element.291), channel_id=1, source_target_pairs={{0,7},{1,0},{2,1},{3,2},{4,3},{5,4},{6,5},{7,6},{8,15},{9,8},{10,9... | collective-permute-start | bytes 786440 | tf_op jit(solution)/shard_map/while/body/eval_jaxpr/ppermute | solution.py:46
  53.9 3.9 %collective-permute-done = f32[512,128]{1,0:T(8,128)S(1)} collective-permute-done((f32[512,128]{1,0:T(8,128)S(1)}, f32[512,128]{1,0:T(8,128)S(1)}, u32[]{:S(2)}, u32[]{:S(2)}) %collective-permute-start) | collective-permute-done | bytes 262176 | tf_op jit(solution)/shard_map/while/body/eval_jaxpr/ppermute | solution.py:46
  58.7 3.0 %while.54 = (s32[]{:T(128)}, f32[64,128]{1,0:T(8,128)S(1)}, f32[512,128]{1,0:T(8,128)S(1)}, f32[64,512]{1,0:T(8,128)S(1)}, pred[64,512]{1,0:T(32,128)(4,1)S(1)}, /*index=5*/s32[]{:T(128)}) while((s32[]{:T(128)}, f32[64,128]{1,0:T(8,128)S(1)}, f32[512,128]{1,0:T(8,128)S(1)}, f32[64,512]{1,0:T(8,128)S(1)}, pred[64,512]{1,0:T(32,128)(4,1)S(1)}, ...), condition=%wide.region_2.2_spmd, body=%wide.region_1.1_spmd.sunk | while | flops 34267136 | bytes 1802309 | solution.py:45
  61.7 3.2 %collective-permute-start = (f32[512,128]{1,0:T(8,128)S(1)}, f32[512,128]{1,0:T(8,128)S(1)}, u32[]{:S(2)}, u32[]{:S(2)}) collective-permute-start(f32[512,128]{1,0:T(8,128)S(1)} %get-tuple-element.291), channel_id=1, source_target_pairs={{0,7},{1,0},{2,1},{3,2},{4,3},{5,4},{6,5},{7,6},{8,15},{9,8},{10,9... | collective-permute-start | bytes 786440 | tf_op jit(solution)/shard_map/while/body/eval_jaxpr/ppermute | solution.py:46
  64.9 3.9 %collective-permute-done = f32[512,128]{1,0:T(8,128)S(1)} collective-permute-done((f32[512,128]{1,0:T(8,128)S(1)}, f32[512,128]{1,0:T(8,128)S(1)}, u32[]{:S(2)}, u32[]{:S(2)}) %collective-permute-start) | collective-permute-done | bytes 262176 | tf_op jit(solution)/shard_map/while/body/eval_jaxpr/ppermute | solution.py:46
  69.8 3.0 %while.54 = (s32[]{:T(128)}, f32[64,128]{1,0:T(8,128)S(1)}, f32[512,128]{1,0:T(8,128)S(1)}, f32[64,512]{1,0:T(8,128)S(1)}, pred[64,512]{1,0:T(32,128)(4,1)S(1)}, /*index=5*/s32[]{:T(128)}) while((s32[]{:T(128)}, f32[64,128]{1,0:T(8,128)S(1)}, f32[512,128]{1,0:T(8,128)S(1)}, f32[64,512]{1,0:T(8,128)S(1)}, pred[64,512]{1,0:T(32,128)(4,1)S(1)}, ...), condition=%wide.region_2.2_spmd, body=%wide.region_1.1_spmd.sunk | while | flops 34267136 | bytes 1802309 | solution.py:45
  72.8 3.2 %collective-permute-start = (f32[512,128]{1,0:T(8,128)S(1)}, f32[512,128]{1,0:T(8,128)S(1)}, u32[]{:S(2)}, u32[]{:S(2)}) collective-permute-start(f32[512,128]{1,0:T(8,128)S(1)} %get-tuple-element.291), channel_id=1, source_target_pairs={{0,7},{1,0},{2,1},{3,2},{4,3},{5,4},{6,5},{7,6},{8,15},{9,8},{10,9... | collective-permute-start | bytes 786440 | tf_op jit(solution)/shard_map/while/body/eval_jaxpr/ppermute | solution.py:46
  76.0 3.9 %collective-permute-done = f32[512,128]{1,0:T(8,128)S(1)} collective-permute-done((f32[512,128]{1,0:T(8,128)S(1)}, f32[512,128]{1,0:T(8,128)S(1)}, u32[]{:S(2)}, u32[]{:S(2)}) %collective-permute-start) | collective-permute-done | bytes 262176 | tf_op jit(solution)/shard_map/while/body/eval_jaxpr/ppermute | solution.py:46
  80.9 3.0 %while.54 = (s32[]{:T(128)}, f32[64,128]{1,0:T(8,128)S(1)}, f32[512,128]{1,0:T(8,128)S(1)}, f32[64,512]{1,0:T(8,128)S(1)}, pred[64,512]{1,0:T(32,128)(4,1)S(1)}, /*index=5*/s32[]{:T(128)}) while((s32[]{:T(128)}, f32[64,128]{1,0:T(8,128)S(1)}, f32[512,128]{1,0:T(8,128)S(1)}, f32[64,512]{1,0:T(8,128)S(1)}, pred[64,512]{1,0:T(32,128)(4,1)S(1)}, ...), condition=%wide.region_2.2_spmd, body=%wide.region_1.1_spmd.sunk | while | flops 34267136 | bytes 1802309 | solution.py:45
  83.9 3.2 %collective-permute-start = (f32[512,128]{1,0:T(8,128)S(1)}, f32[512,128]{1,0:T(8,128)S(1)}, u32[]{:S(2)}, u32[]{:S(2)}) collective-permute-start(f32[512,128]{1,0:T(8,128)S(1)} %get-tuple-element.291), channel_id=1, source_target_pairs={{0,7},{1,0},{2,1},{3,2},{4,3},{5,4},{6,5},{7,6},{8,15},{9,8},{10,9... | collective-permute-start | bytes 786440 | tf_op jit(solution)/shard_map/while/body/eval_jaxpr/ppermute | solution.py:46
  87.1 3.9 %collective-permute-done = f32[512,128]{1,0:T(8,128)S(1)} collective-permute-done((f32[512,128]{1,0:T(8,128)S(1)}, f32[512,128]{1,0:T(8,128)S(1)}, u32[]{:S(2)}, u32[]{:S(2)}) %collective-permute-start) | collective-permute-done | bytes 262176 | tf_op jit(solution)/shard_map/while/body/eval_jaxpr/ppermute | solution.py:46
  92.0 3.0 %while.54 = (s32[]{:T(128)}, f32[64,128]{1,0:T(8,128)S(1)}, f32[512,128]{1,0:T(8,128)S(1)}, f32[64,512]{1,0:T(8,128)S(1)}, pred[64,512]{1,0:T(32,128)(4,1)S(1)}, /*index=5*/s32[]{:T(128)}) while((s32[]{:T(128)}, f32[64,128]{1,0:T(8,128)S(1)}, f32[512,128]{1,0:T(8,128)S(1)}, f32[64,512]{1,0:T(8,128)S(1)}, pred[64,512]{1,0:T(32,128)(4,1)S(1)}, ...), condition=%wide.region_2.2_spmd, body=%wide.region_1.1_spmd.sunk | while | flops 34267136 | bytes 1802309 | solution.py:45
  95.0 3.2 %collective-permute-start = (f32[512,128]{1,0:T(8,128)S(1)}, f32[512,128]{1,0:T(8,128)S(1)}, u32[]{:S(2)}, u32[]{:S(2)}) collective-permute-start(f32[512,128]{1,0:T(8,128)S(1)} %get-tuple-element.291), channel_id=1, source_target_pairs={{0,7},{1,0},{2,1},{3,2},{4,3},{5,4},{6,5},{7,6},{8,15},{9,8},{10,9... | collective-permute-start | bytes 786440 | tf_op jit(solution)/shard_map/while/body/eval_jaxpr/ppermute | solution.py:46
  98.2 3.9 %collective-permute-done = f32[512,128]{1,0:T(8,128)S(1)} collective-permute-done((f32[512,128]{1,0:T(8,128)S(1)}, f32[512,128]{1,0:T(8,128)S(1)}, u32[]{:S(2)}, u32[]{:S(2)}) %collective-permute-start) | collective-permute-done | bytes 262176 | tf_op jit(solution)/shard_map/while/body/eval_jaxpr/ppermute | solution.py:46
  103.0 3.0 %while.54 = (s32[]{:T(128)}, f32[64,128]{1,0:T(8,128)S(1)}, f32[512,128]{1,0:T(8,128)S(1)}, f32[64,512]{1,0:T(8,128)S(1)}, pred[64,512]{1,0:T(32,128)(4,1)S(1)}, /*index=5*/s32[]{:T(128)}) while((s32[]{:T(128)}, f32[64,128]{1,0:T(8,128)S(1)}, f32[512,128]{1,0:T(8,128)S(1)}, f32[64,512]{1,0:T(8,128)S(1)}, pred[64,512]{1,0:T(32,128)(4,1)S(1)}, ...), condition=%wide.region_2.2_spmd, body=%wide.region_1.1_spmd.sunk | while | flops 34267136 | bytes 1802309 | solution.py:45
  106.1 3.2 %collective-permute-start = (f32[512,128]{1,0:T(8,128)S(1)}, f32[512,128]{1,0:T(8,128)S(1)}, u32[]{:S(2)}, u32[]{:S(2)}) collective-permute-start(f32[512,128]{1,0:T(8,128)S(1)} %get-tuple-element.291), channel_id=1, source_target_pairs={{0,7},{1,0},{2,1},{3,2},{4,3},{5,4},{6,5},{7,6},{8,15},{9,8},{10,9... | collective-permute-start | bytes 786440 | tf_op jit(solution)/shard_map/while/body/eval_jaxpr/ppermute | solution.py:46
  109.3 3.9 %collective-permute-done = f32[512,128]{1,0:T(8,128)S(1)} collective-permute-done((f32[512,128]{1,0:T(8,128)S(1)}, f32[512,128]{1,0:T(8,128)S(1)}, u32[]{:S(2)}, u32[]{:S(2)}) %collective-permute-start) | collective-permute-done | bytes 262176 | tf_op jit(solution)/shard_map/while/body/eval_jaxpr/ppermute | solution.py:46
  114.1 3.0 %while.54 = (s32[]{:T(128)}, f32[64,128]{1,0:T(8,128)S(1)}, f32[512,128]{1,0:T(8,128)S(1)}, f32[64,512]{1,0:T(8,128)S(1)}, pred[64,512]{1,0:T(32,128)(4,1)S(1)}, /*index=5*/s32[]{:T(128)}) while((s32[]{:T(128)}, f32[64,128]{1,0:T(8,128)S(1)}, f32[512,128]{1,0:T(8,128)S(1)}, f32[64,512]{1,0:T(8,128)S(1)}, pred[64,512]{1,0:T(32,128)(4,1)S(1)}, ...), condition=%wide.region_2.2_spmd, body=%wide.region_1.1_spmd.sunk | while | flops 34267136 | bytes 1802309 | solution.py:45
  117.2 3.2 %collective-permute-start = (f32[512,128]{1,0:T(8,128)S(1)}, f32[512,128]{1,0:T(8,128)S(1)}, u32[]{:S(2)}, u32[]{:S(2)}) collective-permute-start(f32[512,128]{1,0:T(8,128)S(1)} %get-tuple-element.291), channel_id=1, source_target_pairs={{0,7},{1,0},{2,1},{3,2},{4,3},{5,4},{6,5},{7,6},{8,15},{9,8},{10,9... | collective-permute-start | bytes 786440 | tf_op jit(solution)/shard_map/while/body/eval_jaxpr/ppermute | solution.py:46
  120.3 3.9 %collective-permute-done = f32[512,128]{1,0:T(8,128)S(1)} collective-permute-done((f32[512,128]{1,0:T(8,128)S(1)}, f32[512,128]{1,0:T(8,128)S(1)}, u32[]{:S(2)}, u32[]{:S(2)}) %collective-permute-start) | collective-permute-done | bytes 262176 | tf_op jit(solution)/shard_map/while/body/eval_jaxpr/ppermute | solution.py:46
  125.2 3.0 %while.54 = (s32[]{:T(128)}, f32[64,128]{1,0:T(8,128)S(1)}, f32[512,128]{1,0:T(8,128)S(1)}, f32[64,512]{1,0:T(8,128)S(1)}, pred[64,512]{1,0:T(32,128)(4,1)S(1)}, /*index=5*/s32[]{:T(128)}) while((s32[]{:T(128)}, f32[64,128]{1,0:T(8,128)S(1)}, f32[512,128]{1,0:T(8,128)S(1)}, f32[64,512]{1,0:T(8,128)S(1)}, pred[64,512]{1,0:T(32,128)(4,1)S(1)}, ...), condition=%wide.region_2.2_spmd, body=%wide.region_1.1_spmd.sunk | while | flops 34267136 | bytes 1802309 | solution.py:45
  128.2 3.2 %collective-permute-start = (f32[512,128]{1,0:T(8,128)S(1)}, f32[512,128]{1,0:T(8,128)S(1)}, u32[]{:S(2)}, u32[]{:S(2)}) collective-permute-start(f32[512,128]{1,0:T(8,128)S(1)} %get-tuple-element.291), channel_id=1, source_target_pairs={{0,7},{1,0},{2,1},{3,2},{4,3},{5,4},{6,5},{7,6},{8,15},{9,8},{10,9... | collective-permute-start | bytes 786440 | tf_op jit(solution)/shard_map/while/body/eval_jaxpr/ppermute | solution.py:46
  131.4 3.9 %collective-permute-done = f32[512,128]{1,0:T(8,128)S(1)} collective-permute-done((f32[512,128]{1,0:T(8,128)S(1)}, f32[512,128]{1,0:T(8,128)S(1)}, u32[]{:S(2)}, u32[]{:S(2)}) %collective-permute-start) | collective-permute-done | bytes 262176 | tf_op jit(solution)/shard_map/while/body/eval_jaxpr/ppermute | solution.py:46
  136.3 3.0 %while.54 = (s32[]{:T(128)}, f32[64,128]{1,0:T(8,128)S(1)}, f32[512,128]{1,0:T(8,128)S(1)}, f32[64,512]{1,0:T(8,128)S(1)}, pred[64,512]{1,0:T(32,128)(4,1)S(1)}, /*index=5*/s32[]{:T(128)}) while((s32[]{:T(128)}, f32[64,128]{1,0:T(8,128)S(1)}, f32[512,128]{1,0:T(8,128)S(1)}, f32[64,512]{1,0:T(8,128)S(1)}, pred[64,512]{1,0:T(32,128)(4,1)S(1)}, ...), condition=%wide.region_2.2_spmd, body=%wide.region_1.1_spmd.sunk | while | flops 34267136 | bytes 1802309 | solution.py:45
  139.3 3.2 %collective-permute-start = (f32[512,128]{1,0:T(8,128)S(1)}, f32[512,128]{1,0:T(8,128)S(1)}, u32[]{:S(2)}, u32[]{:S(2)}) collective-permute-start(f32[512,128]{1,0:T(8,128)S(1)} %get-tuple-element.291), channel_id=1, source_target_pairs={{0,7},{1,0},{2,1},{3,2},{4,3},{5,4},{6,5},{7,6},{8,15},{9,8},{10,9... | collective-permute-start | bytes 786440 | tf_op jit(solution)/shard_map/while/body/eval_jaxpr/ppermute | solution.py:46
  142.5 3.9 %collective-permute-done = f32[512,128]{1,0:T(8,128)S(1)} collective-permute-done((f32[512,128]{1,0:T(8,128)S(1)}, f32[512,128]{1,0:T(8,128)S(1)}, u32[]{:S(2)}, u32[]{:S(2)}) %collective-permute-start) | collective-permute-done | bytes 262176 | tf_op jit(solution)/shard_map/while/body/eval_jaxpr/ppermute | solution.py:46
  147.4 3.0 %while.54 = (s32[]{:T(128)}, f32[64,128]{1,0:T(8,128)S(1)}, f32[512,128]{1,0:T(8,128)S(1)}, f32[64,512]{1,0:T(8,128)S(1)}, pred[64,512]{1,0:T(32,128)(4,1)S(1)}, /*index=5*/s32[]{:T(128)}) while((s32[]{:T(128)}, f32[64,128]{1,0:T(8,128)S(1)}, f32[512,128]{1,0:T(8,128)S(1)}, f32[64,512]{1,0:T(8,128)S(1)}, pred[64,512]{1,0:T(32,128)(4,1)S(1)}, ...), condition=%wide.region_2.2_spmd, body=%wide.region_1.1_spmd.sunk | while | flops 34267136 | bytes 1802309 | solution.py:45
  150.4 3.2 %collective-permute-start = (f32[512,128]{1,0:T(8,128)S(1)}, f32[512,128]{1,0:T(8,128)S(1)}, u32[]{:S(2)}, u32[]{:S(2)}) collective-permute-start(f32[512,128]{1,0:T(8,128)S(1)} %get-tuple-element.291), channel_id=1, source_target_pairs={{0,7},{1,0},{2,1},{3,2},{4,3},{5,4},{6,5},{7,6},{8,15},{9,8},{10,9... | collective-permute-start | bytes 786440 | tf_op jit(solution)/shard_map/while/body/eval_jaxpr/ppermute | solution.py:46
  153.6 3.9 %collective-permute-done = f32[512,128]{1,0:T(8,128)S(1)} collective-permute-done((f32[512,128]{1,0:T(8,128)S(1)}, f32[512,128]{1,0:T(8,128)S(1)}, u32[]{:S(2)}, u32[]{:S(2)}) %collective-permute-start) | collective-permute-done | bytes 262176 | tf_op jit(solution)/shard_map/while/body/eval_jaxpr/ppermute | solution.py:46
  158.5 3.0 %while.54 = (s32[]{:T(128)}, f32[64,128]{1,0:T(8,128)S(1)}, f32[512,128]{1,0:T(8,128)S(1)}, f32[64,512]{1,0:T(8,128)S(1)}, pred[64,512]{1,0:T(32,128)(4,1)S(1)}, /*index=5*/s32[]{:T(128)}) while((s32[]{:T(128)}, f32[64,128]{1,0:T(8,128)S(1)}, f32[512,128]{1,0:T(8,128)S(1)}, f32[64,512]{1,0:T(8,128)S(1)}, pred[64,512]{1,0:T(32,128)(4,1)S(1)}, ...), condition=%wide.region_2.2_spmd, body=%wide.region_1.1_spmd.sunk | while | flops 34267136 | bytes 1802309 | solution.py:45
  161.5 3.2 %collective-permute-start = (f32[512,128]{1,0:T(8,128)S(1)}, f32[512,128]{1,0:T(8,128)S(1)}, u32[]{:S(2)}, u32[]{:S(2)}) collective-permute-start(f32[512,128]{1,0:T(8,128)S(1)} %get-tuple-element.291), channel_id=1, source_target_pairs={{0,7},{1,0},{2,1},{3,2},{4,3},{5,4},{6,5},{7,6},{8,15},{9,8},{10,9... | collective-permute-start | bytes 786440 | tf_op jit(solution)/shard_map/while/body/eval_jaxpr/ppermute | solution.py:46
  164.7 3.9 %collective-permute-done = f32[512,128]{1,0:T(8,128)S(1)} collective-permute-done((f32[512,128]{1,0:T(8,128)S(1)}, f32[512,128]{1,0:T(8,128)S(1)}, u32[]{:S(2)}, u32[]{:S(2)}) %collective-permute-start) | collective-permute-done | bytes 262176 | tf_op jit(solution)/shard_map/while/body/eval_jaxpr/ppermute | solution.py:46
  169.5 3.0 %while.54 = (s32[]{:T(128)}, f32[64,128]{1,0:T(8,128)S(1)}, f32[512,128]{1,0:T(8,128)S(1)}, f32[64,512]{1,0:T(8,128)S(1)}, pred[64,512]{1,0:T(32,128)(4,1)S(1)}, /*index=5*/s32[]{:T(128)}) while((s32[]{:T(128)}, f32[64,128]{1,0:T(8,128)S(1)}, f32[512,128]{1,0:T(8,128)S(1)}, f32[64,512]{1,0:T(8,128)S(1)}, pred[64,512]{1,0:T(32,128)(4,1)S(1)}, ...), condition=%wide.region_2.2_spmd, body=%wide.region_1.1_spmd.sunk | while | flops 34267136 | bytes 1802309 | solution.py:45
  172.6 3.2 %collective-permute-start = (f32[512,128]{1,0:T(8,128)S(1)}, f32[512,128]{1,0:T(8,128)S(1)}, u32[]{:S(2)}, u32[]{:S(2)}) collective-permute-start(f32[512,128]{1,0:T(8,128)S(1)} %get-tuple-element.291), channel_id=1, source_target_pairs={{0,7},{1,0},{2,1},{3,2},{4,3},{5,4},{6,5},{7,6},{8,15},{9,8},{10,9... | collective-permute-start | bytes 786440 | tf_op jit(solution)/shard_map/while/body/eval_jaxpr/ppermute | solution.py:46
  175.8 3.9 %collective-permute-done = f32[512,128]{1,0:T(8,128)S(1)} collective-permute-done((f32[512,128]{1,0:T(8,128)S(1)}, f32[512,128]{1,0:T(8,128)S(1)}, u32[]{:S(2)}, u32[]{:S(2)}) %collective-permute-start) | collective-permute-done | bytes 262176 | tf_op jit(solution)/shard_map/while/body/eval_jaxpr/ppermute | solution.py:46
  (314 shorter events, 65.7 us)
Async XLA Ops:
  0.6 1.4 copy-start.1
  0.6 1.4 copy-start.3
  6.1 7.3 %collective-permute-start = (f32[512,128]{1,0:T(8,128)S(1)}, f32[512,128]{1,0:T(8,128)S(1)}, u32[]{:S(2)}, u32[]{:S(2)}) collective-permute-start(f32[512,128]{1,0:T(8,128)S(1)} %get-tuple-element.291), channel_id=1, source_target_pairs={{0,7},{1,0},{2,1},{3,2},{4,3},{5,4},{6,5},{7,6},{8,15},{9,8},{10,9... | collective-permute-start | bytes 786440 | tf_op jit(solution)/shard_map/while/body/eval_jaxpr/ppermute | solution.py:46
  17.4 7.1 %collective-permute-start = (f32[512,128]{1,0:T(8,128)S(1)}, f32[512,128]{1,0:T(8,128)S(1)}, u32[]{:S(2)}, u32[]{:S(2)}) collective-permute-start(f32[512,128]{1,0:T(8,128)S(1)} %get-tuple-element.291), channel_id=1, source_target_pairs={{0,7},{1,0},{2,1},{3,2},{4,3},{5,4},{6,5},{7,6},{8,15},{9,8},{10,9... | collective-permute-start | bytes 786440 | tf_op jit(solution)/shard_map/while/body/eval_jaxpr/ppermute | solution.py:46
  28.5 7.1 %collective-permute-start = (f32[512,128]{1,0:T(8,128)S(1)}, f32[512,128]{1,0:T(8,128)S(1)}, u32[]{:S(2)}, u32[]{:S(2)}) collective-permute-start(f32[512,128]{1,0:T(8,128)S(1)} %get-tuple-element.291), channel_id=1, source_target_pairs={{0,7},{1,0},{2,1},{3,2},{4,3},{5,4},{6,5},{7,6},{8,15},{9,8},{10,9... | collective-permute-start | bytes 786440 | tf_op jit(solution)/shard_map/while/body/eval_jaxpr/ppermute | solution.py:46
  39.6 7.1 %collective-permute-start = (f32[512,128]{1,0:T(8,128)S(1)}, f32[512,128]{1,0:T(8,128)S(1)}, u32[]{:S(2)}, u32[]{:S(2)}) collective-permute-start(f32[512,128]{1,0:T(8,128)S(1)} %get-tuple-element.291), channel_id=1, source_target_pairs={{0,7},{1,0},{2,1},{3,2},{4,3},{5,4},{6,5},{7,6},{8,15},{9,8},{10,9... | collective-permute-start | bytes 786440 | tf_op jit(solution)/shard_map/while/body/eval_jaxpr/ppermute | solution.py:46
  50.7 7.1 %collective-permute-start = (f32[512,128]{1,0:T(8,128)S(1)}, f32[512,128]{1,0:T(8,128)S(1)}, u32[]{:S(2)}, u32[]{:S(2)}) collective-permute-start(f32[512,128]{1,0:T(8,128)S(1)} %get-tuple-element.291), channel_id=1, source_target_pairs={{0,7},{1,0},{2,1},{3,2},{4,3},{5,4},{6,5},{7,6},{8,15},{9,8},{10,9... | collective-permute-start | bytes 786440 | tf_op jit(solution)/shard_map/while/body/eval_jaxpr/ppermute | solution.py:46
  61.7 7.1 %collective-permute-start = (f32[512,128]{1,0:T(8,128)S(1)}, f32[512,128]{1,0:T(8,128)S(1)}, u32[]{:S(2)}, u32[]{:S(2)}) collective-permute-start(f32[512,128]{1,0:T(8,128)S(1)} %get-tuple-element.291), channel_id=1, source_target_pairs={{0,7},{1,0},{2,1},{3,2},{4,3},{5,4},{6,5},{7,6},{8,15},{9,8},{10,9... | collective-permute-start | bytes 786440 | tf_op jit(solution)/shard_map/while/body/eval_jaxpr/ppermute | solution.py:46
  72.8 7.1 %collective-permute-start = (f32[512,128]{1,0:T(8,128)S(1)}, f32[512,128]{1,0:T(8,128)S(1)}, u32[]{:S(2)}, u32[]{:S(2)}) collective-permute-start(f32[512,128]{1,0:T(8,128)S(1)} %get-tuple-element.291), channel_id=1, source_target_pairs={{0,7},{1,0},{2,1},{3,2},{4,3},{5,4},{6,5},{7,6},{8,15},{9,8},{10,9... | collective-permute-start | bytes 786440 | tf_op jit(solution)/shard_map/while/body/eval_jaxpr/ppermute | solution.py:46
  83.9 7.1 %collective-permute-start = (f32[512,128]{1,0:T(8,128)S(1)}, f32[512,128]{1,0:T(8,128)S(1)}, u32[]{:S(2)}, u32[]{:S(2)}) collective-permute-start(f32[512,128]{1,0:T(8,128)S(1)} %get-tuple-element.291), channel_id=1, source_target_pairs={{0,7},{1,0},{2,1},{3,2},{4,3},{5,4},{6,5},{7,6},{8,15},{9,8},{10,9... | collective-permute-start | bytes 786440 | tf_op jit(solution)/shard_map/while/body/eval_jaxpr/ppermute | solution.py:46
  95.0 7.1 %collective-permute-start = (f32[512,128]{1,0:T(8,128)S(1)}, f32[512,128]{1,0:T(8,128)S(1)}, u32[]{:S(2)}, u32[]{:S(2)}) collective-permute-start(f32[512,128]{1,0:T(8,128)S(1)} %get-tuple-element.291), channel_id=1, source_target_pairs={{0,7},{1,0},{2,1},{3,2},{4,3},{5,4},{6,5},{7,6},{8,15},{9,8},{10,9... | collective-permute-start | bytes 786440 | tf_op jit(solution)/shard_map/while/body/eval_jaxpr/ppermute | solution.py:46
  106.1 7.1 %collective-permute-start = (f32[512,128]{1,0:T(8,128)S(1)}, f32[512,128]{1,0:T(8,128)S(1)}, u32[]{:S(2)}, u32[]{:S(2)}) collective-permute-start(f32[512,128]{1,0:T(8,128)S(1)} %get-tuple-element.291), channel_id=1, source_target_pairs={{0,7},{1,0},{2,1},{3,2},{4,3},{5,4},{6,5},{7,6},{8,15},{9,8},{10,9... | collective-permute-start | bytes 786440 | tf_op jit(solution)/shard_map/while/body/eval_jaxpr/ppermute | solution.py:46
  117.2 7.1 %collective-permute-start = (f32[512,128]{1,0:T(8,128)S(1)}, f32[512,128]{1,0:T(8,128)S(1)}, u32[]{:S(2)}, u32[]{:S(2)}) collective-permute-start(f32[512,128]{1,0:T(8,128)S(1)} %get-tuple-element.291), channel_id=1, source_target_pairs={{0,7},{1,0},{2,1},{3,2},{4,3},{5,4},{6,5},{7,6},{8,15},{9,8},{10,9... | collective-permute-start | bytes 786440 | tf_op jit(solution)/shard_map/while/body/eval_jaxpr/ppermute | solution.py:46
  128.2 7.1 %collective-permute-start = (f32[512,128]{1,0:T(8,128)S(1)}, f32[512,128]{1,0:T(8,128)S(1)}, u32[]{:S(2)}, u32[]{:S(2)}) collective-permute-start(f32[512,128]{1,0:T(8,128)S(1)} %get-tuple-element.291), channel_id=1, source_target_pairs={{0,7},{1,0},{2,1},{3,2},{4,3},{5,4},{6,5},{7,6},{8,15},{9,8},{10,9... | collective-permute-start | bytes 786440 | tf_op jit(solution)/shard_map/while/body/eval_jaxpr/ppermute | solution.py:46
  139.3 7.1 %collective-permute-start = (f32[512,128]{1,0:T(8,128)S(1)}, f32[512,128]{1,0:T(8,128)S(1)}, u32[]{:S(2)}, u32[]{:S(2)}) collective-permute-start(f32[512,128]{1,0:T(8,128)S(1)} %get-tuple-element.291), channel_id=1, source_target_pairs={{0,7},{1,0},{2,1},{3,2},{4,3},{5,4},{6,5},{7,6},{8,15},{9,8},{10,9... | collective-permute-start | bytes 786440 | tf_op jit(solution)/shard_map/while/body/eval_jaxpr/ppermute | solution.py:46
  150.4 7.1 %collective-permute-start = (f32[512,128]{1,0:T(8,128)S(1)}, f32[512,128]{1,0:T(8,128)S(1)}, u32[]{:S(2)}, u32[]{:S(2)}) collective-permute-start(f32[512,128]{1,0:T(8,128)S(1)} %get-tuple-element.291), channel_id=1, source_target_pairs={{0,7},{1,0},{2,1},{3,2},{4,3},{5,4},{6,5},{7,6},{8,15},{9,8},{10,9... | collective-permute-start | bytes 786440 | tf_op jit(solution)/shard_map/while/body/eval_jaxpr/ppermute | solution.py:46
  161.5 7.1 %collective-permute-start = (f32[512,128]{1,0:T(8,128)S(1)}, f32[512,128]{1,0:T(8,128)S(1)}, u32[]{:S(2)}, u32[]{:S(2)}) collective-permute-start(f32[512,128]{1,0:T(8,128)S(1)} %get-tuple-element.291), channel_id=1, source_target_pairs={{0,7},{1,0},{2,1},{3,2},{4,3},{5,4},{6,5},{7,6},{8,15},{9,8},{10,9... | collective-permute-start | bytes 786440 | tf_op jit(solution)/shard_map/while/body/eval_jaxpr/ppermute | solution.py:46
  172.6 7.1 %collective-permute-start = (f32[512,128]{1,0:T(8,128)S(1)}, f32[512,128]{1,0:T(8,128)S(1)}, u32[]{:S(2)}, u32[]{:S(2)}) collective-permute-start(f32[512,128]{1,0:T(8,128)S(1)} %get-tuple-element.291), channel_id=1, source_target_pairs={{0,7},{1,0},{2,1},{3,2},{4,3},{5,4},{6,5},{7,6},{8,15},{9,8},{10,9... | collective-permute-start | bytes 786440 | tf_op jit(solution)/shard_map/while/body/eval_jaxpr/ppermute | solution.py:46
  179.7 0.7 copy-start
  179.7 0.7 copy-start.2
where the time goes:
time: 181 us; the launch traced here: 180 us
  waiting for transfers between devices  61.9 us (34%)
  starting transfers between devices  51.2 us (28%)
  matrix products  43.9 us (24%)
  local copies, waits for them, and re-layouts  17.4 us (10%)
  loops' own time  3.93 us (2%)
    ppermute x16, waiting for transfers between devices, stratum(): item_blk = lax.ppermute(item_blk, 'shard', shift_back)  61.9 us
    ppermute x16, starting transfers between devices, stratum(): item_blk = lax.ppermute(item_blk, 'shard', shift_back)  51.2 us
    dot_general x64, matrix products, step(): jnp.einsum('ui,ur->ir', residual, user_bf, preferred_element_type=jnp.flo...  25 us
    dot_general x64, matrix products, step(): grad_user = jnp.dot(residual, item_bf, preferred_element_type=jnp.float32)  18.9 us
    dynamic_slice x16, local copies, waits for them, and re-layouts, stratum(): rating_blk = lax.dynamic_slice_in_dim(ratings, col_start, items_dev, axis=1)  14.7 us
  transfers between devices with their start and end apart: 16, of which 16 were waited for; matrix products, arithmetic and copies ran while one was open for 0% of the time, Pallas kernels for 0%

commit v1 on v0

v1 whole, which is shorter than its diff:
```python
import functools
import math

import jax
import jax.numpy as jnp
from jax import lax
from jax.experimental import pallas as pl
from jax.experimental.pallas import tpu as pltpu
from jax.sharding import PartitionSpec as P

STRATUM_STEPS = 4
EPOCHS = 2
MESH = pl.DeviceIdType.MESH
F32 = jnp.float32
BF16 = jnp.bfloat16


def kernel(
    n, eta, lam, r_ref, m_ref, u_ref, v_ref, uo_ref, vo_ref,
    rp, rin, ubuf, vt, rsend, rrecv, usend, urecv,
):
    users, rank = u_ref.shape
    items = v_ref.shape[0]
    me = lax.axis_index("shard")
    right = lax.rem(me + 1, n)
    keep = 1.0 - eta * lam

    barrier = pltpu.get_barrier_semaphore()
    for d in range(1, n):
        pl.semaphore_signal(barrier, inc=1, device_id={"shard": lax.rem(me + d, n)}, device_id_type=MESH)

    for t in range(n):
        j = lax.rem(me + t, n)
        cols = pl.ds(pl.multiple_of(j * items, items), items)
        blk = jnp.where(m_ref[:, cols] != 0, r_ref[:, cols], jnp.inf)
        if t == 0:
            rin[0] = blk
        else:
            rp[t - 1] = blk
    vt[...] = v_ref[...].T
    ubuf[0] = u_ref[...]

    pl.semaphore_wait(barrier, n - 1)

    def r_copy(t):
        return pltpu.make_async_remote_copy(
            src_ref=rp.at[t - 1], dst_ref=rin.at[t], send_sem=rsend.at[t - 1], recv_sem=rrecv.at[t - 1],
            device_id={"shard": lax.rem(me + t, n)}, device_id_type=MESH,
        )

    def u_copy(s):
        return pltpu.make_async_remote_copy(
            src_ref=ubuf.at[s], dst_ref=ubuf.at[s + 1], send_sem=usend.at[s], recv_sem=urecv.at[s],
            device_id={"shard": right}, device_id_type=MESH,
        )

    for t in range(1, n):
        r_copy(t).start()

    def residual(ub, vb, t):
        pred = jnp.dot(ub, vb, preferred_element_type=F32)
        rat = rin[t]
        return jnp.where(rat < jnp.inf, pred - rat, 0.0).astype(BF16)

    def user_step(u, t):
        vb = vt[...].astype(BF16)
        err = residual(u.astype(BF16), vb, t)
        grad = lax.dot_general(err, vb, (((1,), (1,)), ((), ())), preferred_element_type=F32)
        return keep * u - eta * grad

    def item_step(u, t):
        v = vt[...]
        ub = u.astype(BF16)
        err = residual(ub, v.astype(BF16), t)
        grad = jnp.dot(u.T.astype(BF16), err, preferred_element_type=F32)
        vt[...] = keep * v - eta * grad

    def stratum(s, t):
        u = user_step(ubuf[s], t)

        def pair(_, u):
            item_step(u, t)
            return user_step(u, t)

        u = lax.fori_loop(0, STRATUM_STEPS - 1, pair, u)
        ubuf[s] = u
        u_copy(s).start()
        item_step(u, t)
        u_copy(s).wait()

    def first_epoch(s, carry):
        stratum(s, s)

        @pl.when(s + 1 < n)
        def _():
            r_copy(s + 1).wait()

        return carry

    def later_epoch(s, carry):
        stratum(s, lax.rem(s, n))
        return carry

    lax.fori_loop(0, n, first_epoch, 0)
    lax.fori_loop(n, EPOCHS * n, later_epoch, 0)
    uo_ref[...] = ubuf[EPOCHS * n]
    vo_ref[...] = vt[...].T


def solution(mesh):
    n = mesh.shape["shard"]
    row_spec = P(("rep", "shard"), None)

    def local(ratings, observed, user_init, item_init):
        users, rank = user_init.shape
        items = item_init.shape[0]
        scale = (users + items + rank) / math.sqrt(rank)
        eta = 0.5 / scale
        lam = 0.03 * math.sqrt(users * items / rank)
        vm = pl.BlockSpec(memory_space=pltpu.VMEM)
        steps = EPOCHS * n
        return pl.pallas_call(
            functools.partial(kernel, n, eta, lam),
            out_shape=(
                jax.ShapeDtypeStruct(user_init.shape, F32),
                jax.ShapeDtypeStruct(item_init.shape, F32),
            ),
            in_specs=[vm] * 4,
            out_specs=(vm, vm),
            scratch_shapes=[
                pltpu.VMEM((n - 1, users, items), F32),
                pltpu.VMEM((n, users, items), F32),
                pltpu.VMEM((steps + 1, users, rank), F32),
                pltpu.VMEM((rank, items), F32),
                pltpu.SemaphoreType.DMA((n - 1,)),
                pltpu.SemaphoreType.DMA((n - 1,)),
                pltpu.SemaphoreType.DMA((steps,)),
                pltpu.SemaphoreType.DMA((steps,)),
            ],
            compiler_params=pltpu.CompilerParams(collective_id=0, has_side_effects=True),
        )(ratings, observed, user_init, item_init)

    return jax.shard_map(local, mesh=mesh, in_specs=(row_spec,) * 4, out_specs=(row_spec, row_spec), check_vma=False)
```

time: 181 us -> 81.5 us (0.45)
  the two profiles are of different devices: /device:TPU:112 before, /device:TPU:113 now
where the time goes in v1:
time: 81.5 us; the launch traced here: 81.3 us
  Pallas kernels  77.6 us (95%)
  local copies, waits for them, and re-layouts  3.04 us (4%)
    pallas_call x1, Pallas kernels, local(): pl.pallas_call(functools.partial(kernel, n, eta, lam), out_shape=(jax.Sha...  77.6 us
    unnamed x2, local copies, waits for them, and re-layouts  3.04 us

profile of v1, /device:TPU:113, one launch (start us, length us, event | category | flops | bytes accessed | tf_op | source)
XLA Modules:
  0.0 81.3 jit_solution(13163418836359390996)
XLA Ops:
  0.6 77.6 %shard_map.59 = (f32[64,128]{1,0:T(8,128)}, f32[512,128]{1,0:T(8,128)}) custom-call(f32[64,4096]{1,0:T(8,128)} %r_ref.1, s32[64,4096]{1,0:T(8,128)} %m_ref.1, f32[64,128]{1,0:T(8,128)} %u_ref.1, f32[512,128]{1,0:T(8,128)} %v_ref.1), custom_call_target="tpu_custom_call" | custom-call | tf_op jit(solution)/shard_map/pallas_call | solution.py:122
  78.3 1.4 %copy.8 = f32[64,128]{1,0:T(8,128)} copy(f32[64,128]{1,0:T(8,128)} %get-tuple-element.4) | data formatting | bytes 65536
  79.6 1.7 %copy.9 = f32[512,128]{1,0:T(8,128)} copy(f32[512,128]{1,0:T(8,128)} %get-tuple-element.5) | data formatting | bytes 524288

commit v2 on v1

--- a/solution.py
+++ b/solution.py
@@ -17,7 +17,7 @@
 
 def kernel(
     n, eta, lam, r_ref, m_ref, u_ref, v_ref, uo_ref, vo_ref,
-    rp, rin, ubuf, vt, rsend, rrecv, usend, urecv,
+    rbuf, mbuf, vbuf, rp, rin, ubuf, vt, rload, mload, uvload, rsend, rrecv, usend, urecv,
 ):
     users, rank = u_ref.shape
     items = v_ref.shape[0]
@@ -25,22 +25,22 @@
     right = lax.rem(me + 1, n)
     keep = 1.0 - eta * lam
 
-    barrier = pltpu.get_barrier_semaphore()
-    for d in range(1, n):
-        pl.semaphore_signal(barrier, inc=1, device_id={"shard": lax.rem(me + d, n)}, device_id_type=MESH)
+    def cols(t):
+        return pl.ds(pl.multiple_of(lax.rem(me + t, n) * items, items), items)
 
-    for t in range(n):
-        j = lax.rem(me + t, n)
-        cols = pl.ds(pl.multiple_of(j * items, items), items)
-        blk = jnp.where(m_ref[:, cols] != 0, r_ref[:, cols], jnp.inf)
-        if t == 0:
-            rin[0] = blk
-        else:
-            rp[t - 1] = blk
-    vt[...] = v_ref[...].T
-    ubuf[0] = u_ref[...]
+    def r_load(t):
+        return pltpu.make_async_copy(r_ref.at[:, cols(t)], rbuf.at[t], rload.at[t])
 
-    pl.semaphore_wait(barrier, n - 1)
+    def m_load(t):
+        return pltpu.make_async_copy(m_ref.at[:, cols(t)], mbuf.at[t], mload.at[t])
+
+    u_load = pltpu.make_async_copy(u_ref, ubuf.at[0], uvload.at[0])
+    v_load = pltpu.make_async_copy(v_ref, vbuf, uvload.at[1])
+
+    def masked(t):
+        r_load(t).wait()
+        m_load(t).wait()
+        return jnp.where(mbuf[t] != 0, rbuf[t], jnp.inf)
 
     def r_copy(t):
         return pltpu.make_async_remote_copy(
@@ -54,8 +54,23 @@
             device_id={"shard": right}, device_id_type=MESH,
         )
 
-    for t in range(1, n):
-        r_copy(t).start()
+    v_load.start()
+    u_load.start()
+    for t in range(n):
+        r_load(t).start()
+        m_load(t).start()
+
+    barrier = pltpu.get_barrier_semaphore()
+    for d in range(1, n):
+        pl.semaphore_signal(barrier, inc=1, device_id={"shard": lax.rem(me + d, n)}, device_id_type=MESH)
+
+    v_load.wait()
+    vt[...] = vbuf[...].T
+    u_load.wait()
+    rin[0] = masked(0)
+    rp[0] = masked(1)
+    pl.semaphore_wait(barrier, n - 1)
+    r_copy(1).start()
 
     def residual(ub, vb, t):
         pred = jnp.dot(ub, vb, preferred_element_type=F32)
@@ -75,34 +90,40 @@
         grad = jnp.dot(u.T.astype(BF16), err, preferred_element_type=F32)
         vt[...] = keep * v - eta * grad
 
-    def stratum(s, t):
+    def stratum(s, t, after_send):
         u = user_step(ubuf[s], t)
-
-        def pair(_, u):
+        for _ in range(STRATUM_STEPS - 1):
             item_step(u, t)
-            return user_step(u, t)
-
-        u = lax.fori_loop(0, STRATUM_STEPS - 1, pair, u)
+            u = user_step(u, t)
         ubuf[s] = u
         u_copy(s).start()
+        after_send()
         item_step(u, t)
         u_copy(s).wait()
 
     def first_epoch(s, carry):
-        stratum(s, s)
+        def send_ahead():
+            @pl.when(s + 2 < n)
+            def _():
+                rp[s + 1] = masked(s + 2)
+                r_copy(s + 2).start()
+
+        stratum(s, s, send_ahead)
 
         @pl.when(s + 1 < n)
         def _():
-            r_copy(s + 1).wait()
+            r_copy(s + 1).wait_recv()
 
         return carry
 
     def later_epoch(s, carry):
-        stratum(s, lax.rem(s, n))
+        stratum(s, lax.rem(s, n), lambda: None)
         return carry
 
     lax.fori_loop(0, n, first_epoch, 0)
     lax.fori_loop(n, EPOCHS * n, later_epoch, 0)
+    for t in range(1, n):
+        r_copy(t).wait_send()
     uo_ref[...] = ubuf[EPOCHS * n]
     vo_ref[...] = vt[...].T
 
@@ -117,21 +138,24 @@
         scale = (users + items + rank) / math.sqrt(rank)
         eta = 0.5 / scale
         lam = 0.03 * math.sqrt(users * items / rank)
-        vm = pl.BlockSpec(memory_space=pltpu.VMEM)
+        vmem = pl.BlockSpec(memory_space=pltpu.VMEM)
         steps = EPOCHS * n
         return pl.pallas_call(
             functools.partial(kernel, n, eta, lam),
-            out_shape=(
-                jax.ShapeDtypeStruct(user_init.shape, F32),
-                jax.ShapeDtypeStruct(item_init.shape, F32),
-            ),
-            in_specs=[vm] * 4,
-            out_specs=(vm, vm),
+            out_shape=(pltpu.VMEM(user_init.shape, F32), pltpu.VMEM(item_init.shape, F32)),
+            in_specs=[pl.BlockSpec(memory_space=pltpu.HBM)] * 4,
+            out_specs=(vmem, vmem),
             scratch_shapes=[
+                pltpu.VMEM((n, users, items), F32),
+                pltpu.VMEM((n, users, items), jnp.int32),
+                pltpu.VMEM((items, rank), F32),
                 pltpu.VMEM((n - 1, users, items), F32),
                 pltpu.VMEM((n, users, items), F32),
                 pltpu.VMEM((steps + 1, users, rank), F32),
                 pltpu.VMEM((rank, items), F32),
+                pltpu.SemaphoreType.DMA((n,)),
+                pltpu.SemaphoreType.DMA((n,)),
+                pltpu.SemaphoreType.DMA((2,)),
                 pltpu.SemaphoreType.DMA((n - 1,)),
                 pltpu.SemaphoreType.DMA((n - 1,)),
                 pltpu.SemaphoreType.DMA((steps,)),

time: 81.5 us -> 68.3 us (0.84)
  Pallas kernels: 77.6 us -> 65.8 us
  local copies, waits for them, and re-layouts: 3.04 us -> 1.32 us
    pallas_call x1, Pallas kernels: 77.6 us -> 65.8 us  [local(): pl.pallas_call(functools.partial(kernel, n, eta, lam), out_shape=(pltpu.V...]
    unnamed x2, local copies, waits for them, and re-layouts: 3.04 us -> 1.32 us
where the time goes in v2:
time: 68.3 us; the launch traced here: 67.7 us
  Pallas kernels  65.8 us (96%)
  local copies, waits for them, and re-layouts  1.32 us (2%)
    pallas_call x1, Pallas kernels, local(): pl.pallas_call(functools.partial(kernel, n, eta, lam), out_shape=(pltpu.V...  65.8 us

profile of v2, /device:TPU:113, one launch (start us, length us, event | category | flops | bytes accessed | tf_op | source)
XLA Modules:
  0.0 67.7 jit_solution(11155536347243734087)
XLA Ops:
  0.6 65.8 %shard_map.59 = (f32[64,128]{1,0:T(8,128)S(1)}, f32[512,128]{1,0:T(8,128)S(1)}) custom-call(f32[64,4096]{1,0:T(8,128)} %r_ref.1, s32[64,4096]{1,0:T(8,128)} %m_ref.1, f32[64,128]{1,0:T(8,128)} %u_ref.1, f32[512,128]{1,0:T(8,128)} %v_ref.1), custom_call_target="tpu_custom_call" | custom-call | tf_op jit(solution)/shard_map/pallas_call | solution.py:143
  66.4 0.6 copy.8
  67.0 0.7 %copy.9 = f32[512,128]{1,0:T(8,128)} copy(f32[512,128]{1,0:T(8,128)S(1)} %get-tuple-element.3) | data formatting | bytes 524288

commit v3 on v2

v3 whole, which is shorter than its diff:
```python
import functools
import math

import jax
import jax.numpy as jnp
from jax import lax
from jax.experimental import pallas as pl
from jax.experimental.pallas import tpu as pltpu
from jax.sharding import PartitionSpec as P

EPOCHS = 2
MESH = pl.DeviceIdType.MESH
F32 = jnp.float32
BF16 = jnp.bfloat16
A, B = 0, 1


def kernel(
    n, eta, lam, r_ref, m_ref, u_ref, v_ref, uo_ref, vo_ref,
    rbuf, mbuf, vbuf, rp, rin, uin, uout, ucur, vt, vhome,
    rload, mload, uvload, rsend, rrecv, usend, urecv, vsend, vrecv, pace,
):
    items = v_ref.shape[0]
    steps = EPOCHS * n
    me = lax.axis_index("shard")
    worker = lax.rem(me, 2) == 1
    keep = 1.0 - eta * lam

    def dev(offset):
        return {"shard": lax.rem(me + n + offset, n)}

    barrier = pltpu.get_barrier_semaphore()
    for d in range(1, n):
        pl.semaphore_signal(barrier, inc=1, device_id=dev(d), device_id_type=MESH)

    def cols(t):
        return pl.ds(pl.multiple_of(lax.rem(me + t, n) * items, items), items)

    def r_load(t):
        return pltpu.make_async_copy(r_ref.at[:, cols(t)], rbuf.at[t], rload.at[t])

    def m_load(t):
        return pltpu.make_async_copy(m_ref.at[:, cols(t)], mbuf.at[t], mload.at[t])

    u_load = pltpu.make_async_copy(u_ref, ucur, uvload.at[0])
    v_load = pltpu.make_async_copy(v_ref, vbuf, uvload.at[1])

    def load(ts):
        for t in ts:
            r_load(t).start()
            m_load(t).start()

    def masked(t):
        r_load(t).wait()
        m_load(t).wait()
        return jnp.where(mbuf[t] != 0, rbuf[t], jnp.inf)

    def remote(src, dst, send, recv, device):
        return pltpu.make_async_remote_copy(
            src_ref=src, dst_ref=dst, send_sem=send, recv_sem=recv, device_id=device, device_id_type=MESH
        )

    def r_copy(t):
        j = lax.rem(me + t, n)
        chain = lax.rem(j, 2)
        return remote(rp.at[t], rin.at[chain, t], rsend.at[t], rrecv.at[chain, t], {"shard": j - chain + 1})

    def r_arrive(chain, t):
        remote(rp.at[t], rin.at[chain, t], rsend.at[t], rrecv.at[chain, t], dev(1)).wait_recv()

    def u_copy(s, offset=2):
        return remote(uout.at[s], uin.at[s + 1], usend.at[s], urecv.at[s + 1], dev(offset))

    def u_arrive(s):
        remote(ucur, uin.at[s], usend.at[0], urecv.at[s], dev(1)).wait_recv()

    u_first = remote(ucur, uin.at[0], usend.at[0], urecv.at[0], dev(1))
    v_first = remote(vt.at[A], vt.at[A], vsend, vrecv, dev(1))
    v_last = remote(vt.at[A], vhome, vsend, vrecv, dev(-1))

    def residual(ub, vb, chain, t):
        pred = jnp.dot(ub, vb, preferred_element_type=F32)
        rat = rin[chain, t]
        return jnp.where(rat < jnp.inf, pred - rat, 0.0).astype(BF16)

    def user_step(u, chain, t):
        vb = vt[chain].astype(BF16)
        err = residual(u.astype(BF16), vb, chain, t)
        grad = lax.dot_general(err, vb, (((1,), (1,)), ((), ())), preferred_element_type=F32)
        return keep * u - eta * grad

    def item_step(u, chain, t):
        v = vt[chain]
        err = residual(u.astype(BF16), v.astype(BF16), chain, t)
        grad = jnp.dot(u.T.astype(BF16), err, preferred_element_type=F32)
        vt[chain] = keep * v - eta * grad

    def send_ahead(s):
        @pl.when(s + 2 < n - 1)
        def _():
            rp[s + 2] = masked(s + 2)
            r_copy(s + 2).start()

        @pl.when(s + 2 == n - 1)
        def _():
            rin[A, n - 1] = masked(n - 1)

        @pl.when(s + 2 < n)
        def _():
            pl.semaphore_signal(pace, inc=1, device_id=dev(-1), device_id_type=MESH)

    def begin(u, t):
        u = user_step(u, B, t)
        item_step(u, B, t)
        u = user_step(u, B, t)
        ucur[...] = u
        item_step(u, B, t)

    def stratum(s, first, last=False):
        t = s if first else lax.rem(s, n)
        u_arrive(s)
        if first:
            @pl.when(s < n - 1)
            def _():
                r_arrive(A, s)

        a = uin[s]
        b = ucur[...]
        a = user_step(a, A, t)
        b = user_step(b, B, t)
        item_step(a, A, t)
        item_step(b, B, t)
        a = user_step(a, A, t)
        b = user_step(b, B, t)
        uout[s] = b
        u_copy(s, 1 if last else 2).start()
        if first:
            send_ahead(s)
        item_step(a, A, t)
        item_step(b, B, t)
        a = user_step(a, A, t)
        item_step(a, A, t)
        a = user_step(a, A, t)
        if last:
            item_step(a, A, t)
            ucur[...] = a
            return
        if first:
            @pl.when(s < n - 1)
            def _():
                r_arrive(B, s + 1)

        t_next = lax.rem(s + 1, n)
        b = user_step(a, B, t_next)
        item_step(a, A, t)
        item_step(b, B, t_next)
        b = user_step(b, B, t_next)
        ucur[...] = b
        item_step(b, B, t_next)

    @pl.when(worker)
    def _():
        v_load.start()
        u_load.start()
        load(range(2))
        v_load.wait()
        vt[B] = vbuf[...].T
        u_load.wait()
        rin[B, 0] = masked(0)
        rp[1] = masked(1)
        load(range(2, n))
        pl.semaphore_wait(barrier, n - 1)
        r_copy(1).start()
        begin(ucur[...], 0)
        v_first.wait_recv()

        def first_epoch(s, carry):
            stratum(s, True)
            return carry

        def later_epoch(s, carry):
            stratum(s, False)
            return carry

        lax.fori_loop(0, n, first_epoch, 0)
        lax.fori_loop(n, steps - 1, later_epoch, 0)
        stratum(steps - 1, False, last=True)
        v_last.start()
        vo_ref[...] = vt[B].T
        uo_ref[...] = ucur[...]
        for t in range(1, n - 1):
            r_copy(t).wait_send()
        for s in range(steps):
            u_copy(s).wait_send()
        v_last.wait_send()

    @pl.when(jnp.logical_not(worker))
    def _():
        v_load.start()
        u_load.start()
        load(range(2))
        v_load.wait()
        vt[A] = vbuf[...].T
        u_load.wait()
        rp[0] = masked(0)
        rp[1] = masked(1)
        load(range(2, n))
        pl.semaphore_wait(barrier, n - 1)
        v_first.start()
        u_first.start()
        r_copy(0).start()
        r_copy(1).start()

        def send(t, carry):
            rp[t] = masked(t)
            pl.semaphore_wait(pace, 1)
            r_copy(t).start()
            return carry

        lax.fori_loop(2, n, send, 0)
        for t in range(n):
            r_copy(t).wait_send()
        u_first.wait_send()
        v_first.wait_send()
        u_arrive(steps)
        uo_ref[...] = uin[steps]
        v_last.wait_recv()
        vo_ref[...] = vhome[...].T


def write_out(u_ref, v_ref, uo_ref, vo_ref, sems):
    copies = [pltpu.make_async_copy(v_ref, vo_ref, sems.at[0]), pltpu.make_async_copy(u_ref, uo_ref, sems.at[1])]
    for c in copies:
        c.start()
    for c in copies:
        c.wait()


def solution(mesh):
    n = mesh.shape["shard"]
    row_spec = P(("rep", "shard"), None)

    def local(ratings, observed, user_init, item_init):
        users, rank = user_init.shape
        items = item_init.shape[0]
        scale = (users + items + rank) / math.sqrt(rank)
        eta = 0.5 / scale
        lam = 0.03 * math.sqrt(users * items / rank)
        steps = EPOCHS * n
        vmem = pl.BlockSpec(memory_space=pltpu.VMEM)
        hbm = pl.BlockSpec(memory_space=pltpu.HBM)
        dma = pltpu.SemaphoreType.DMA
        u_last, v_last = pl.pallas_call(
            functools.partial(kernel, n, eta, lam),
            out_shape=(pltpu.VMEM(user_init.shape, F32), pltpu.VMEM(item_init.shape, F32)),
            in_specs=[hbm] * 4,
            out_specs=(vmem, vmem),
            scratch_shapes=[
                pltpu.VMEM((n, users, items), F32),
                pltpu.VMEM((n, users, items), jnp.int32),
                pltpu.VMEM((items, rank), F32),
                pltpu.VMEM((n, users, items), F32),
                pltpu.VMEM((2, n, users, items), F32),
                pltpu.VMEM((steps + 1, users, rank), F32),
                pltpu.VMEM((steps, users, rank), F32),
                pltpu.VMEM((users, rank), F32),
                pltpu.VMEM((2, rank, items), F32),
                pltpu.VMEM((rank, items), F32),
                dma((n,)),
                dma((n,)),
                dma((2,)),
                dma((n,)),
                dma((2, n)),
                dma((steps,)),
                dma((steps + 1,)),
                dma,
                dma,
                pltpu.SemaphoreType.REGULAR,
            ],
            compiler_params=pltpu.CompilerParams(collective_id=0, has_side_effects=True),
        )(ratings, observed, user_init, item_init)
        return pl.pallas_call(
            write_out,
            out_shape=(jax.ShapeDtypeStruct(user_init.shape, F32), jax.ShapeDtypeStruct(item_init.shape, F32)),
            in_specs=[vmem] * 2,
            out_specs=(hbm, hbm),
            scratch_shapes=[dma((2,))],
            compiler_params=pltpu.CompilerParams(vmem_limit_bytes=2**20),
        )(u_last, v_last)

    return jax.shard_map(local, mesh=mesh, in_specs=(row_spec,) * 4, out_specs=(row_spec, row_spec), check_vma=False)
```

time: 68.3 us -> 65.1 us (0.953)
  Pallas kernels: 65.8 us -> 64.3 us
  local copies, waits for them, and re-layouts: 1.32 us -> 0 us
    pallas_call x1, Pallas kernels: 65.8 us -> 63.6 us  [local(): pl.pallas_call(functools.partial(kernel, n, eta, lam), out_shape=(pltpu.V...]
    unnamed x2 -> x0, local copies, waits for them, and re-layouts: 1.32 us -> none
    pallas_call x0 -> x1, Pallas kernels: none -> 0.72 us  [local(): pl.pallas_call(write_out, out_shape=(jax.ShapeDtypeStruct(user_init.shape...]
where the time goes in v3:
time: 65.1 us; the launch traced here: 64.9 us
  Pallas kernels  64.3 us (99%)
    pallas_call x1, Pallas kernels, local(): pl.pallas_call(functools.partial(kernel, n, eta, lam), out_shape=(pltpu.V...  63.6 us

profile of v3, /device:TPU:113, one launch (start us, length us, event | category | flops | bytes accessed | tf_op | source)
XLA Modules:
  0.0 64.9 jit_solution(4430396184885175138)
XLA Ops:
  0.6 63.6 %shard_map.59 = (f32[64,128]{1,0:T(8,128)S(1)}, f32[512,128]{1,0:T(8,128)S(1)}) custom-call(f32[64,4096]{1,0:T(8,128)} %r_ref.1, s32[64,4096]{1,0:T(8,128)} %m_ref.1, f32[64,128]{1,0:T(8,128)} %u_ref.1, f32[512,128]{1,0:T(8,128)} %v_ref.1), custom_call_target="tpu_custom_call" | custom-call | tf_op jit(solution)/shard_map/pallas_call | solution.py:253
  64.2 0.7 %shard_map.60 = (f32[64,128]{1,0:T(8,128)}, f32[512,128]{1,0:T(8,128)}) custom-call(f32[64,128]{1,0:T(8,128)S(1)} %get-tuple-element.4.u_ref, f32[512,128]{1,0:T(8,128)S(1)} %get-tuple-element.5.v_ref), custom_call_target="tpu_custom_call" | custom-call | tf_op jit(solution)/shard_map/pallas_call | solution.py:282

commit v4 on v3

--- a/solution.py
+++ b/solution.py
@@ -12,6 +12,7 @@
 MESH = pl.DeviceIdType.MESH
 F32 = jnp.float32
 BF16 = jnp.bfloat16
+TILE = 256
 A, B = 0, 1
 
 
@@ -78,22 +79,44 @@
     v_first = remote(vt.at[A], vt.at[A], vsend, vrecv, dev(1))
     v_last = remote(vt.at[A], vhome, vsend, vrecv, dev(-1))
 
-    def residual(ub, vb, chain, t):
-        pred = jnp.dot(ub, vb, preferred_element_type=F32)
-        rat = rin[chain, t]
-        return jnp.where(rat < jnp.inf, pred - rat, 0.0).astype(BF16)
-
-    def user_step(u, chain, t):
-        vb = vt[chain].astype(BF16)
-        err = residual(u.astype(BF16), vb, chain, t)
-        grad = lax.dot_general(err, vb, (((1,), (1,)), ((), ())), preferred_element_type=F32)
-        return keep * u - eta * grad
-
-    def item_step(u, chain, t):
-        v = vt[chain]
-        err = residual(u.astype(BF16), v.astype(BF16), chain, t)
-        grad = jnp.dot(u.T.astype(BF16), err, preferred_element_type=F32)
-        vt[chain] = keep * v - eta * grad
+    def tile(k):
+        return pl.ds(k * TILE, TILE)
+
+    class Chain:
+        def __init__(self, chain, t, u):
+            self.chain, self.t, self.u = chain, t, u
+
+        def predict(self):
+            ub = self.u.astype(BF16)
+            self.err = []
+            for k in range(items // TILE):
+                pred = jnp.dot(ub, vt[self.chain, :, tile(k)].astype(BF16), preferred_element_type=F32)
+                rat = rin[self.chain, self.t, :, tile(k)]
+                self.err.append(jnp.where(rat < jnp.inf, pred - rat, 0.0).astype(BF16))
+
+        def users(self):
+            new = keep * self.u
+            for k in range(items // TILE):
+                vb = vt[self.chain, :, tile(k)].astype(BF16)
+                grad = lax.dot_general(self.err[k], vb, (((1,), (1,)), ((), ())), preferred_element_type=F32)
+                new = new - eta * grad
+            self.u = new
+
+        def items(self):
+            ut = self.u.T.astype(BF16)
+            for k in range(items // TILE):
+                grad = jnp.dot(ut, self.err[k], preferred_element_type=F32)
+                vt[self.chain, :, tile(k)] = keep * vt[self.chain, :, tile(k)] - eta * grad
+
+    def advance(order, **work):
+        queue = {}
+        for name, (chain, kinds) in work.items():
+            queue[name] = []
+            for kind in kinds:
+                queue[name] += [chain.predict, chain.users if kind == "u" else chain.items]
+        for name in order:
+            queue[name].pop(0)()
+        assert not any(queue.values())
 
     def send_ahead(s):
         @pl.when(s + 2 < n - 1)
@@ -105,16 +128,13 @@
         def _():
             rin[A, n - 1] = masked(n - 1)
 
-        @pl.when(s + 2 < n)
-        def _():
-            pl.semaphore_signal(pace, inc=1, device_id=dev(-1), device_id_type=MESH)
 
     def begin(u, t):
-        u = user_step(u, B, t)
-        item_step(u, B, t)
-        u = user_step(u, B, t)
-        ucur[...] = u
-        item_step(u, B, t)
+        b = Chain(B, t, u)
+        advance("bbbb", b=(b, "uv"))
+        advance("bb", b=(b, "u"))
+        ucur[...] = b.u
+        advance("bb", b=(b, "v"))
 
     def stratum(s, first, last=False):
         t = s if first else lax.rem(s, n)
@@ -124,39 +144,27 @@
             def _():
                 r_arrive(A, s)
 
-        a = uin[s]
-        b = ucur[...]
-        a = user_step(a, A, t)
-        b = user_step(b, B, t)
-        item_step(a, A, t)
-        item_step(b, B, t)
-        a = user_step(a, A, t)
-        b = user_step(b, B, t)
-        uout[s] = b
+        a = Chain(A, t, uin[s])
+        b = Chain(B, t, ucur[...])
+        advance("abababababab", a=(a, "uvu"), b=(b, "uvu"))
+        uout[s] = b.u
         u_copy(s, 1 if last else 2).start()
         if first:
             send_ahead(s)
-        item_step(a, A, t)
-        item_step(b, B, t)
-        a = user_step(a, A, t)
-        item_step(a, A, t)
-        a = user_step(a, A, t)
+        advance("ababaaaaaa", a=(a, "vuvu"), b=(b, "v"))
         if last:
-            item_step(a, A, t)
-            ucur[...] = a
+            advance("aa", a=(a, "v"))
+            ucur[...] = a.u
             return
         if first:
             @pl.when(s < n - 1)
             def _():
                 r_arrive(B, s + 1)
 
-        t_next = lax.rem(s + 1, n)
-        b = user_step(a, B, t_next)
-        item_step(a, A, t)
-        item_step(b, B, t_next)
-        b = user_step(b, B, t_next)
-        ucur[...] = b
-        item_step(b, B, t_next)
+        b = Chain(B, lax.rem(s + 1, n), a.u)
+        advance("bababbbb", a=(a, "v"), b=(b, "uvu"))
+        ucur[...] = b.u
+        advance("bb", b=(b, "v"))
 
     @pl.when(worker)
     def _():
@@ -210,15 +218,17 @@
         u_first.start()
         r_copy(0).start()
         r_copy(1).start()
+        rp[2] = masked(2)
+        r_copy(2).start()
 
         def send(t, carry):
             rp[t] = masked(t)
-            pl.semaphore_wait(pace, 1)
+            r_copy(t - 1).wait_send()
             r_copy(t).start()
             return carry
 
-        lax.fori_loop(2, n, send, 0)
-        for t in range(n):
+        lax.fori_loop(3, n, send, 0)
+        for t in (0, 1, n - 1):
             r_copy(t).wait_send()
         u_first.wait_send()
         v_first.wait_send()

time: 65.1 us -> 60.1 us (0.923)
  Pallas kernels: 64.3 us -> 59.4 us
    pallas_call x1, Pallas kernels: 63.6 us -> 58.6 us  [local(): pl.pallas_call(functools.partial(kernel, n, eta, lam), out_shape=(pltpu.V...]
where the time goes in v4:
time: 60.1 us; the launch traced here: 60 us
  Pallas kernels  59.4 us (99%)
  between operations  0.64 us (1%)
    pallas_call x1, Pallas kernels, local(): pl.pallas_call(functools.partial(kernel, n, eta, lam), out_shape=(pltpu.V...  58.6 us

profile of v4, /device:TPU:113, one launch (start us, length us, event | category | flops | bytes accessed | tf_op | source)
XLA Modules:
  0.0 60.0 jit_solution(584851621792981434)
XLA Ops:
  0.6 58.6 %shard_map.59 = (f32[64,128]{1,0:T(8,128)S(1)}, f32[512,128]{1,0:T(8,128)S(1)}) custom-call(f32[64,4096]{1,0:T(8,128)} %r_ref.1, s32[64,4096]{1,0:T(8,128)} %m_ref.1, f32[64,128]{1,0:T(8,128)} %u_ref.1, f32[512,128]{1,0:T(8,128)} %v_ref.1), custom_call_target="tpu_custom_call" | custom-call | tf_op jit(solution)/shard_map/pallas_call | solution.py:263
  59.3 0.7 %shard_map.60 = (f32[64,128]{1,0:T(8,128)}, f32[512,128]{1,0:T(8,128)}) custom-call(f32[64,128]{1,0:T(8,128)S(1)} %get-tuple-element.4.u_ref, f32[512,128]{1,0:T(8,128)S(1)} %get-tuple-element.5.v_ref), custom_call_target="tpu_custom_call" | custom-call | tf_op jit(solution)/shard_map/pallas_call | solution.py:292

commit v5 on v4

--- a/solution.py
+++ b/solution.py
@@ -18,8 +18,8 @@
 
 def kernel(
     n, eta, lam, r_ref, m_ref, u_ref, v_ref, uo_ref, vo_ref,
-    rbuf, mbuf, vbuf, rp, rin, uin, uout, ucur, vt, vhome,
-    rload, mload, uvload, rsend, rrecv, usend, urecv, vsend, vrecv, pace,
+    rbuf, mbuf, rall, mall, vbuf, rp, rin, uin, uout, ucur, vt, vhome,
+    rload, mload, allload, uvload, rsend, rrecv, usend, urecv, vsend, vrecv, pace,
 ):
     items = v_ref.shape[0]
     steps = EPOCHS * n
@@ -31,8 +31,10 @@
         return {"shard": lax.rem(me + n + offset, n)}
 
     barrier = pltpu.get_barrier_semaphore()
-    for d in range(1, n):
-        pl.semaphore_signal(barrier, inc=1, device_id=dev(d), device_id_type=MESH)
+
+    def greet(*offsets):
+        for d in offsets:
+            pl.semaphore_signal(barrier, inc=1, device_id=dev(d), device_id_type=MESH)
 
     def cols(t):
         return pl.ds(pl.multiple_of(lax.rem(me + t, n) * items, items), items)
@@ -46,15 +48,30 @@
     u_load = pltpu.make_async_copy(u_ref, ucur, uvload.at[0])
     v_load = pltpu.make_async_copy(v_ref, vbuf, uvload.at[1])
 
-    def load(ts):
-        for t in ts:
+    r_all = pltpu.make_async_copy(r_ref, rall, allload.at[0])
+    m_all = pltpu.make_async_copy(m_ref, mall, allload.at[1])
+
+    def start_loads():
+        v_load.start()
+        u_load.start()
+        for t in range(2):
             r_load(t).start()
             m_load(t).start()
 
+    def start_rest():
+        r_all.start()
+        m_all.start()
+
+    def wait_all():
+        r_all.wait()
+        m_all.wait()
+
     def masked(t):
-        r_load(t).wait()
-        m_load(t).wait()
-        return jnp.where(mbuf[t] != 0, rbuf[t], jnp.inf)
+        if isinstance(t, int) and t < 2:
+            r_load(t).wait()
+            m_load(t).wait()
+            return jnp.where(mbuf[t] != 0, rbuf[t], jnp.inf)
+        return jnp.where(mall[:, cols(t)] != 0, rall[:, cols(t)], jnp.inf)
 
     def remote(src, dst, send, recv, device):
         return pltpu.make_async_remote_copy(
@@ -118,20 +135,33 @@
             queue[name].pop(0)()
         assert not any(queue.values())
 
+    ahead = [[2, n - 2], [3], list(range(4, n - 2))]
+
     def send_ahead(s):
-        @pl.when(s + 2 < n - 1)
+        @pl.when(s == 0)
         def _():
-            rp[s + 2] = masked(s + 2)
-            r_copy(s + 2).start()
-
-        @pl.when(s + 2 == n - 1)
+            wait_all()
+
+        for k, blocks in enumerate(ahead):
+            @pl.when(s == k)
+            def _():
+                for t in blocks:
+                    rp[t] = masked(t)
+                    r_copy(t).start()
+
+        @pl.when(s == len(ahead))
         def _():
             rin[A, n - 1] = masked(n - 1)
 
-
-    def begin(u, t):
+    def enter():
+        pl.semaphore_wait(barrier, n // 2 + 1)
+        r_copy(1).start()
+        pl.semaphore_signal(pace, inc=1, device_id=dev(-1), device_id_type=MESH)
+
+    def begin(u, t, enter):
         b = Chain(B, t, u)
         advance("bbbb", b=(b, "uv"))
+        enter()
         advance("bb", b=(b, "u"))
         ucur[...] = b.u
         advance("bb", b=(b, "v"))
@@ -168,18 +198,15 @@
 
     @pl.when(worker)
     def _():
-        v_load.start()
-        u_load.start()
-        load(range(2))
+        greet(-1, *range(2, n, 2))
+        start_loads()
         v_load.wait()
         vt[B] = vbuf[...].T
         u_load.wait()
         rin[B, 0] = masked(0)
         rp[1] = masked(1)
-        load(range(2, n))
-        pl.semaphore_wait(barrier, n - 1)
-        r_copy(1).start()
-        begin(ucur[...], 0)
+        start_rest()
+        begin(ucur[...], 0, enter)
         v_first.wait_recv()
 
         def first_epoch(s, carry):
@@ -204,30 +231,27 @@
 
     @pl.when(jnp.logical_not(worker))
     def _():
-        v_load.start()
-        u_load.start()
-        load(range(2))
+        greet(1, -1)
+        start_loads()
         v_load.wait()
         vt[A] = vbuf[...].T
+        pl.semaphore_wait(barrier, 1)
+        v_first.start()
         u_load.wait()
+        u_first.start()
         rp[0] = masked(0)
+        r_copy(0).start()
         rp[1] = masked(1)
-        load(range(2, n))
-        pl.semaphore_wait(barrier, n - 1)
-        v_first.start()
-        u_first.start()
-        r_copy(0).start()
         r_copy(1).start()
-        rp[2] = masked(2)
+        start_rest()
+        wait_all()
+        for t in range(2, n):
+            rp[t] = masked(t)
+        pl.semaphore_wait(pace, 1)
         r_copy(2).start()
-
-        def send(t, carry):
-            rp[t] = masked(t)
+        for t in range(3, n):
             r_copy(t - 1).wait_send()
             r_copy(t).start()
-            return carry
-
-        lax.fori_loop(3, n, send, 0)
         for t in (0, 1, n - 1):
             r_copy(t).wait_send()
         u_first.wait_send()
@@ -266,8 +290,10 @@
             in_specs=[hbm] * 4,
             out_specs=(vmem, vmem),
             scratch_shapes=[
-                pltpu.VMEM((n, users, items), F32),
-                pltpu.VMEM((n, users, items), jnp.int32),
+                pltpu.VMEM((2, users, items), F32),
+                pltpu.VMEM((2, users, items), jnp.int32),
+                pltpu.VMEM(ratings.shape, F32),
+                pltpu.VMEM(observed.shape, jnp.int32),
                 pltpu.VMEM((items, rank), F32),
                 pltpu.VMEM((n, users, items), F32),
                 pltpu.VMEM((2, n, users, items), F32),
@@ -276,8 +302,9 @@
                 pltpu.VMEM((users, rank), F32),
                 pltpu.VMEM((2, rank, items), F32),
                 pltpu.VMEM((rank, items), F32),
-                dma((n,)),
-                dma((n,)),
+                dma((2,)),
+                dma((2,)),
+                dma((2,)),
                 dma((2,)),
                 dma((n,)),
                 dma((2, n)),

time: 60.1 us -> 59.2 us (0.985)
  Pallas kernels: 59.4 us -> 58.4 us
    pallas_call x1, Pallas kernels: 58.6 us -> 57.7 us  [local(): pl.pallas_call(functools.partial(kernel, n, eta, lam), out_shape=(pltpu.V...]
where the time goes in v5:
time: 59.2 us; the launch traced here: 59.1 us
  Pallas kernels  58.4 us (99%)
  between operations  0.64 us (1%)
    pallas_call x1, Pallas kernels, local(): pl.pallas_call(functools.partial(kernel, n, eta, lam), out_shape=(pltpu.V...  57.7 us

profile of v5, /device:TPU:113, one launch (start us, length us, event | category | flops | bytes accessed | tf_op | source)
XLA Modules:
  0.0 59.1 jit_solution(16757440350005382407)
XLA Ops:
  0.6 57.7 %shard_map.59 = (f32[64,128]{1,0:T(8,128)S(1)}, f32[512,128]{1,0:T(8,128)S(1)}) custom-call(f32[64,4096]{1,0:T(8,128)} %r_ref.1, s32[64,4096]{1,0:T(8,128)} %m_ref.1, f32[64,128]{1,0:T(8,128)} %u_ref.1, f32[512,128]{1,0:T(8,128)} %v_ref.1), custom_call_target="tpu_custom_call" | custom-call | tf_op jit(solution)/shard_map/pallas_call | solution.py:287
  58.4 0.7 %shard_map.60 = (f32[64,128]{1,0:T(8,128)}, f32[512,128]{1,0:T(8,128)}) custom-call(f32[64,128]{1,0:T(8,128)S(1)} %get-tuple-element.4.u_ref, f32[512,128]{1,0:T(8,128)S(1)} %get-tuple-element.5.v_ref), custom_call_target="tpu_custom_call" | custom-call | tf_op jit(solution)/shard_map/pallas_call | solution.py:319

commit v6 on v5

--- a/solution.py
+++ b/solution.py
@@ -78,21 +78,21 @@
             src_ref=src, dst_ref=dst, send_sem=send, recv_sem=recv, device_id=device, device_id_type=MESH
         )
 
-    def r_copy(t):
+    def r_copy(t, slot=0):
         j = lax.rem(me + t, n)
         chain = lax.rem(j, 2)
-        return remote(rp.at[t], rin.at[chain, t], rsend.at[t], rrecv.at[chain, t], {"shard": j - chain + 1})
+        return remote(rp.at[t], rin.at[chain, t], rsend.at[slot], rrecv.at[chain, t], {"shard": j - chain + 1})
 
     def r_arrive(chain, t):
-        remote(rp.at[t], rin.at[chain, t], rsend.at[t], rrecv.at[chain, t], dev(1)).wait_recv()
+        remote(rp.at[t], rin.at[chain, t], rsend.at[0], rrecv.at[chain, t], dev(1)).wait_recv()
 
     def u_copy(s, offset=2):
-        return remote(uout.at[s], uin.at[s + 1], usend.at[s], urecv.at[s + 1], dev(offset))
+        return remote(uout.at[s], uin.at[s + 1], usend, urecv.at[(s + 1) % n], dev(offset))
 
     def u_arrive(s):
-        remote(ucur, uin.at[s], usend.at[0], urecv.at[s], dev(1)).wait_recv()
-
-    u_first = remote(ucur, uin.at[0], usend.at[0], urecv.at[0], dev(1))
+        remote(ucur, uin.at[s], usend, urecv.at[s % n], dev(1)).wait_recv()
+
+    u_first = remote(ucur, uin.at[0], usend, urecv.at[0], dev(1))
     v_first = remote(vt.at[A], vt.at[A], vsend, vrecv, dev(1))
     v_last = remote(vt.at[A], vhome, vsend, vrecv, dev(-1))
 
@@ -138,20 +138,22 @@
     ahead = [[2, n - 2], [3], list(range(4, n - 2))]
 
     def send_ahead(s):
-        @pl.when(s == 0)
+        @pl.when(s <= len(ahead))
         def _():
-            wait_all()
-
-        for k, blocks in enumerate(ahead):
-            @pl.when(s == k)
+            @pl.when(s == 0)
             def _():
-                for t in blocks:
-                    rp[t] = masked(t)
-                    r_copy(t).start()
-
-        @pl.when(s == len(ahead))
-        def _():
-            rin[A, n - 1] = masked(n - 1)
+                wait_all()
+
+            for k, blocks in enumerate(ahead):
+                @pl.when(s == k)
+                def _():
+                    for t in blocks:
+                        rp[t] = masked(t)
+                        r_copy(t).start()
+
+            @pl.when(s == len(ahead))
+            def _():
+                rin[A, n - 1] = masked(n - 1)
 
     def enter():
         pl.semaphore_wait(barrier, n // 2 + 1)
@@ -170,9 +172,7 @@
         t = s if first else lax.rem(s, n)
         u_arrive(s)
         if first:
-            @pl.when(s < n - 1)
-            def _():
-                r_arrive(A, s)
+            r_arrive(A, s)
 
         a = Chain(A, t, uin[s])
         b = Chain(B, t, ucur[...])
@@ -187,9 +187,7 @@
             ucur[...] = a.u
             return
         if first:
-            @pl.when(s < n - 1)
-            def _():
-                r_arrive(B, s + 1)
+            r_arrive(B, s + 1)
 
         b = Chain(B, lax.rem(s + 1, n), a.u)
         advance("bababbbb", a=(a, "v"), b=(b, "uvu"))
@@ -217,16 +215,15 @@
             stratum(s, False)
             return carry
 
-        lax.fori_loop(0, n, first_epoch, 0)
-        lax.fori_loop(n, steps - 1, later_epoch, 0)
+        lax.fori_loop(0, n - 1, first_epoch, 0)
+        lax.fori_loop(n - 1, steps - 1, later_epoch, 0)
         stratum(steps - 1, False, last=True)
         v_last.start()
         vo_ref[...] = vt[B].T
         uo_ref[...] = ucur[...]
-        for t in range(1, n - 1):
-            r_copy(t).wait_send()
-        for s in range(steps):
-            u_copy(s).wait_send()
+        sent = rp.at[pl.ds(1, n - 2)]
+        pltpu.make_async_copy(sent, sent, rsend.at[0]).wait()
+        pltpu.make_async_copy(uout, uout, usend).wait()
         v_last.wait_send()
 
     @pl.when(jnp.logical_not(worker))
@@ -240,20 +237,21 @@
         u_load.wait()
         u_first.start()
         rp[0] = masked(0)
-        r_copy(0).start()
+        r_copy(0, 1).start()
         rp[1] = masked(1)
-        r_copy(1).start()
+        r_copy(1, 2).start()
         start_rest()
         wait_all()
         for t in range(2, n):
             rp[t] = masked(t)
+        r_copy(0, 1).wait_send()
         pl.semaphore_wait(pace, 1)
-        r_copy(2).start()
+        r_copy(2, 1).start()
+        r_copy(1, 2).wait_send()
         for t in range(3, n):
-            r_copy(t - 1).wait_send()
-            r_copy(t).start()
-        for t in (0, 1, n - 1):
-            r_copy(t).wait_send()
+            r_copy(t - 1, 1 + (t - 1) % 2).wait_send()
+            r_copy(t, 1 + t % 2).start()
+        r_copy(n - 1, 1 + (n - 1) % 2).wait_send()
         u_first.wait_send()
         v_first.wait_send()
         u_arrive(steps)
@@ -306,10 +304,10 @@
                 dma((2,)),
                 dma((2,)),
                 dma((2,)),
+                dma((3,)),
+                dma((2, n)),
+                dma,
                 dma((n,)),
-                dma((2, n)),
-                dma((steps,)),
-                dma((steps + 1,)),
                 dma,
                 dma,
                 pltpu.SemaphoreType.REGULAR,

time: 59.2 us -> 58.9 us (level)
  no operation moved by 1% of the time
where the time goes in v6:
time: 58.9 us; the launch traced here: 58.7 us
  Pallas kernels  58.1 us (99%)
  between operations  0.64 us (1%)
    pallas_call x1, Pallas kernels, local(): pl.pallas_call(functools.partial(kernel, n, eta, lam), out_shape=(pltpu.V...  57.4 us

profile of v6, /device:TPU:113, one launch (start us, length us, event | category | flops | bytes accessed | tf_op | source)
XLA Modules:
  0.0 58.7 jit_solution(5719601973252538991)
XLA Ops:
  0.6 57.4 %shard_map.59 = (f32[64,128]{1,0:T(8,128)S(1)}, f32[512,128]{1,0:T(8,128)S(1)}) custom-call(f32[64,4096]{1,0:T(8,128)} %r_ref.1, s32[64,4096]{1,0:T(8,128)} %m_ref.1, f32[64,128]{1,0:T(8,128)} %u_ref.1, f32[512,128]{1,0:T(8,128)} %v_ref.1), custom_call_target="tpu_custom_call" | custom-call | tf_op jit(solution)/shard_map/pallas_call | solution.py:285
  58.0 0.7 %shard_map.60 = (f32[64,128]{1,0:T(8,128)}, f32[512,128]{1,0:T(8,128)}) custom-call(f32[64,128]{1,0:T(8,128)S(1)} %get-tuple-element.4.u_ref, f32[512,128]{1,0:T(8,128)S(1)} %get-tuple-element.5.v_ref), custom_call_target="tpu_custom_call" | custom-call | tf_op jit(solution)/shard_map/pallas_call | solution.py:317

commit v7 on v6

--- a/solution.py
+++ b/solution.py
@@ -87,10 +87,10 @@
         remote(rp.at[t], rin.at[chain, t], rsend.at[0], rrecv.at[chain, t], dev(1)).wait_recv()
 
     def u_copy(s, offset=2):
-        return remote(uout.at[s], uin.at[s + 1], usend, urecv.at[(s + 1) % n], dev(offset))
+        return remote(uout.at[s], uin.at[s + 1], usend, urecv.at[lax.rem(s + 1, n)], dev(offset))
 
     def u_arrive(s):
-        remote(ucur, uin.at[s], usend, urecv.at[s % n], dev(1)).wait_recv()
+        remote(ucur, uin.at[s], usend, urecv.at[lax.rem(s, n)], dev(1)).wait_recv()
 
     u_first = remote(ucur, uin.at[0], usend, urecv.at[0], dev(1))
     v_first = remote(vt.at[A], vt.at[A], vsend, vrecv, dev(1))
@@ -181,7 +181,7 @@
         u_copy(s, 1 if last else 2).start()
         if first:
             send_ahead(s)
-        advance("ababaaaaaa", a=(a, "vuvu"), b=(b, "v"))
+        advance("aaababaaaa", a=(a, "vuvu"), b=(b, "v"))
         if last:
             advance("aa", a=(a, "v"))
             ucur[...] = a.u

time: 58.9 us -> 58.7 us (level)
  no operation moved by 1% of the time
where the time goes in v7:
time: 58.7 us; the launch traced here: 58.6 us
  Pallas kernels  58 us (99%)
  between operations  0.64 us (1%)
    pallas_call x1, Pallas kernels, local(): pl.pallas_call(functools.partial(kernel, n, eta, lam), out_shape=(pltpu.V...  57.2 us

profile of v7, /device:TPU:113, one launch (start us, length us, event | category | flops | bytes accessed | tf_op | source)
XLA Modules:
  0.0 58.6 jit_solution(16695665733239570139)
XLA Ops:
  0.6 57.2 %shard_map.59 = (f32[64,128]{1,0:T(8,128)S(1)}, f32[512,128]{1,0:T(8,128)S(1)}) custom-call(f32[64,4096]{1,0:T(8,128)} %r_ref.1, s32[64,4096]{1,0:T(8,128)} %m_ref.1, f32[64,128]{1,0:T(8,128)} %u_ref.1, f32[512,128]{1,0:T(8,128)} %v_ref.1), custom_call_target="tpu_custom_call" | custom-call | tf_op jit(solution)/shard_map/pallas_call | solution.py:285
  57.9 0.7 %shard_map.60 = (f32[64,128]{1,0:T(8,128)}, f32[512,128]{1,0:T(8,128)}) custom-call(f32[64,128]{1,0:T(8,128)S(1)} %get-tuple-element.4.u_ref, f32[512,128]{1,0:T(8,128)S(1)} %get-tuple-element.5.v_ref), custom_call_target="tpu_custom_call" | custom-call | tf_op jit(solution)/shard_map/pallas_call | solution.py:317

commit v8 on v7

--- a/solution.py
+++ b/solution.py
@@ -105,11 +105,10 @@
 
         def predict(self):
             ub = self.u.astype(BF16)
-            self.err = []
-            for k in range(items // TILE):
-                pred = jnp.dot(ub, vt[self.chain, :, tile(k)].astype(BF16), preferred_element_type=F32)
-                rat = rin[self.chain, self.t, :, tile(k)]
-                self.err.append(jnp.where(rat < jnp.inf, pred - rat, 0.0).astype(BF16))
+            pred = jnp.dot(ub, vt[self.chain].astype(BF16), preferred_element_type=F32)
+            rat = rin[self.chain, self.t]
+            err = jnp.where(rat < jnp.inf, pred - rat, 0.0).astype(BF16)
+            self.err = [err[:, k * TILE:(k + 1) * TILE] for k in range(items // TILE)]
 
         def users(self):
             new = keep * self.u
@@ -156,6 +155,7 @@
                 rin[A, n - 1] = masked(n - 1)
 
     def enter():
+        rp[1] = masked(1)
         pl.semaphore_wait(barrier, n // 2 + 1)
         r_copy(1).start()
         pl.semaphore_signal(pace, inc=1, device_id=dev(-1), device_id_type=MESH)
@@ -202,7 +202,6 @@
         vt[B] = vbuf[...].T
         u_load.wait()
         rin[B, 0] = masked(0)
-        rp[1] = masked(1)
         start_rest()
         begin(ucur[...], 0, enter)
         v_first.wait_recv()

time: 58.7 us -> 58.7 us (level)
  no operation moved by 1% of the time
where the time goes in v8:
time: 58.7 us; the launch traced here: 58.6 us
  Pallas kernels  57.9 us (99%)
  between operations  0.64 us (1%)
    pallas_call x1, Pallas kernels, local(): pl.pallas_call(functools.partial(kernel, n, eta, lam), out_shape=(pltpu.V...  57.2 us

profile of v8, /device:TPU:113, one launch (start us, length us, event | category | flops | bytes accessed | tf_op | source)
XLA Modules:
  0.0 58.6 jit_solution(9969523511214867491)
XLA Ops:
  0.6 57.2 %shard_map.59 = (f32[64,128]{1,0:T(8,128)S(1)}, f32[512,128]{1,0:T(8,128)S(1)}) custom-call(f32[64,4096]{1,0:T(8,128)} %r_ref.1, s32[64,4096]{1,0:T(8,128)} %m_ref.1, f32[64,128]{1,0:T(8,128)} %u_ref.1, f32[512,128]{1,0:T(8,128)} %v_ref.1), custom_call_target="tpu_custom_call" | custom-call | tf_op jit(solution)/shard_map/pallas_call | solution.py:284
  57.8 0.7 %shard_map.60 = (f32[64,128]{1,0:T(8,128)}, f32[512,128]{1,0:T(8,128)}) custom-call(f32[64,128]{1,0:T(8,128)S(1)} %get-tuple-element.4.u_ref, f32[512,128]{1,0:T(8,128)S(1)} %get-tuple-element.5.v_ref), custom_call_target="tpu_custom_call" | custom-call | tf_op jit(solution)/shard_map/pallas_call | solution.py:316

commit v9 on v8

--- a/solution.py
+++ b/solution.py
@@ -19,7 +19,7 @@
 def kernel(
     n, eta, lam, r_ref, m_ref, u_ref, v_ref, uo_ref, vo_ref,
     rbuf, mbuf, rall, mall, vbuf, rp, rin, uin, uout, ucur, vt, vhome,
-    rload, mload, allload, uvload, rsend, rrecv, usend, urecv, vsend, vrecv, pace,
+    rload, allload, uvload, rsend, rrecv, usend, urecv, vsend, vrecv, pace,
 ):
     items = v_ref.shape[0]
     steps = EPOCHS * n
@@ -43,13 +43,13 @@
         return pltpu.make_async_copy(r_ref.at[:, cols(t)], rbuf.at[t], rload.at[t])
 
     def m_load(t):
-        return pltpu.make_async_copy(m_ref.at[:, cols(t)], mbuf.at[t], mload.at[t])
+        return pltpu.make_async_copy(m_ref.at[:, cols(t)], mbuf.at[t], rload.at[t])
 
     u_load = pltpu.make_async_copy(u_ref, ucur, uvload.at[0])
     v_load = pltpu.make_async_copy(v_ref, vbuf, uvload.at[1])
 
-    r_all = pltpu.make_async_copy(r_ref, rall, allload.at[0])
-    m_all = pltpu.make_async_copy(m_ref, mall, allload.at[1])
+    r_all = pltpu.make_async_copy(r_ref, rall, allload)
+    m_all = pltpu.make_async_copy(m_ref, mall, allload)
 
     def start_loads():
         v_load.start()
@@ -63,13 +63,12 @@
         m_all.start()
 
     def wait_all():
-        r_all.wait()
-        m_all.wait()
+        pltpu.make_async_copy(rin, rin, allload).wait()
 
     def masked(t):
         if isinstance(t, int) and t < 2:
-            r_load(t).wait()
-            m_load(t).wait()
+            pair = rin.at[0, pl.ds(0, 2)]
+            pltpu.make_async_copy(pair, pair, rload.at[t]).wait()
             return jnp.where(mbuf[t] != 0, rbuf[t], jnp.inf)
         return jnp.where(mall[:, cols(t)] != 0, rall[:, cols(t)], jnp.inf)
 
@@ -300,8 +299,7 @@
                 pltpu.VMEM((2, rank, items), F32),
                 pltpu.VMEM((rank, items), F32),
                 dma((2,)),
-                dma((2,)),
-                dma((2,)),
+                dma,
                 dma((2,)),
                 dma((3,)),
                 dma((2, n)),

time: 58.7 us -> 58.8 us (level)
  no operation moved by 1% of the time
where the time goes in v9:
time: 58.8 us; the launch traced here: 58.7 us
  Pallas kernels  58 us (99%)
  between operations  0.64 us (1%)
    pallas_call x1, Pallas kernels, local(): pl.pallas_call(functools.partial(kernel, n, eta, lam), out_shape=(pltpu.V...  57.3 us

profile of v9, /device:TPU:113, one launch (start us, length us, event | category | flops | bytes accessed | tf_op | source)
XLA Modules:
  0.0 58.7 jit_solution(10791659929704195290)
XLA Ops:
  0.6 57.3 %shard_map.59 = (f32[64,128]{1,0:T(8,128)S(1)}, f32[512,128]{1,0:T(8,128)S(1)}) custom-call(f32[64,4096]{1,0:T(8,128)} %r_ref.1, s32[64,4096]{1,0:T(8,128)} %m_ref.1, f32[64,128]{1,0:T(8,128)} %u_ref.1, f32[512,128]{1,0:T(8,128)} %v_ref.1), custom_call_target="tpu_custom_call" | custom-call | tf_op jit(solution)/shard_map/pallas_call | solution.py:283
  57.9 0.7 %shard_map.60 = (f32[64,128]{1,0:T(8,128)}, f32[512,128]{1,0:T(8,128)}) custom-call(f32[64,128]{1,0:T(8,128)S(1)} %get-tuple-element.4.u_ref, f32[512,128]{1,0:T(8,128)S(1)} %get-tuple-element.5.v_ref), custom_call_target="tpu_custom_call" | custom-call | tf_op jit(solution)/shard_map/pallas_call | solution.py:314

commit v10 on v8

--- a/solution.py
+++ b/solution.py
@@ -181,7 +181,7 @@
         u_copy(s, 1 if last else 2).start()
         if first:
             send_ahead(s)
-        advance("aaababaaaa", a=(a, "vuvu"), b=(b, "v"))
+        advance("aaaababaaa", a=(a, "vuvu"), b=(b, "v"))
         if last:
             advance("aa", a=(a, "v"))
             ucur[...] = a.u

time: 58.7 us -> 58.8 us (level)
  no operation moved by 1% of the time
where the time goes in v10:
time: 58.8 us; the launch traced here: 58.7 us
  Pallas kernels  58 us (99%)
  between operations  0.64 us (1%)
    pallas_call x1, Pallas kernels, local(): pl.pallas_call(functools.partial(kernel, n, eta, lam), out_shape=(pltpu.V...  57.3 us

profile of v10, /device:TPU:113, one launch (start us, length us, event | category | flops | bytes accessed | tf_op | source)
XLA Modules:
  0.0 58.7 jit_solution(10745842797111579341)
XLA Ops:
  0.6 57.3 %shard_map.59 = (f32[64,128]{1,0:T(8,128)S(1)}, f32[512,128]{1,0:T(8,128)S(1)}) custom-call(f32[64,4096]{1,0:T(8,128)} %r_ref.1, s32[64,4096]{1,0:T(8,128)} %m_ref.1, f32[64,128]{1,0:T(8,128)} %u_ref.1, f32[512,128]{1,0:T(8,128)} %v_ref.1), custom_call_target="tpu_custom_call" | custom-call | tf_op jit(solution)/shard_map/pallas_call | solution.py:284
  58.0 0.7 %shard_map.60 = (f32[64,128]{1,0:T(8,128)}, f32[512,128]{1,0:T(8,128)}) custom-call(f32[64,128]{1,0:T(8,128)S(1)} %get-tuple-element.4.u_ref, f32[512,128]{1,0:T(8,128)S(1)} %get-tuple-element.5.v_ref), custom_call_target="tpu_custom_call" | custom-call | tf_op jit(solution)/shard_map/pallas_call | solution.py:316
